TPU v7x, 8 devices: a whole 2x2x1 slice. The times are simulated.
8 devices in a mesh: dp: 2 (over z, y), cp: 4 (over x, core).
Axes of the slice: x: 2, y: 2, z: 1, core: 2. Of those that a mesh axis runs over, the one named last changes fastest.
Arguments:
- vis_feat: bfloat16 [16, 4096, 1152], P(('dp', 'cp')), parts along dimension 0
- text_emb: bfloat16 [8192, 2560], P(('dp', 'cp')), parts along dimension 0
- img_pos: int32 [16], P('dp'), parts along dimension 0
- grad_y: bfloat16 [8192, 2560], P(('dp', 'cp')), parts along dimension 0
- pn_gain: bfloat16 [1152], replicated
- w_proj: bfloat16 [1152, 2560], replicated
- pre_gain: bfloat16 [2560], replicated
- w_query: bfloat16 [2560, 2048], replicated
- w_key: bfloat16 [2560, 1024], replicated
- w_value: bfloat16 [2560, 1024], replicated
- q_gain: bfloat16 [256], replicated
- k_gain: bfloat16 [256], replicated
- w_out: bfloat16 [2048, 2560], replicated
- post_gain: bfloat16 [2560], replicated
Outputs:
- output 1: bfloat16 [8192, 2560], P(('dp', 'cp')), parts along dimension 0
- output 2: bfloat16 [8192, 2560], P(('dp', 'cp')), parts along dimension 0
- output 3: bfloat16 [16, 4096, 1152], P(('dp', 'cp')), parts along dimension 0
- output 4: bfloat16 [2304], P('dp'), parts along dimension 0
- output 5: bfloat16 [2304, 2560], P('dp'), parts along dimension 0
- output 6: bfloat16 [5120], P('dp'), parts along dimension 0
- output 7: bfloat16 [5120, 2048], P('dp'), parts along dimension 0
- output 8: bfloat16 [5120, 1024], P('dp'), parts along dimension 0
- output 9: bfloat16 [5120, 1024], P('dp'), parts along dimension 0
- output 10: bfloat16 [512], P('dp'), parts along dimension 0
- output 11: bfloat16 [512], P('dp'), parts along dimension 0
- output 12: bfloat16 [4096, 2560], P('dp'), parts along dimension 0
- output 13: bfloat16 [5120], P('dp'), parts along dimension 0
There are 2 independent parts. A program takes and returns all parts, laid end to end along the dimension named above; an argument that names none is the same for every part.
All inputs are finite; a program needn't handle non-finite values.
Results may differ from a plain program's by a relative error of at most 0.02.
Values are sent between devices in bfloat16 or wider.
A program may use at most 1 GiB of HBM per device.

v0:
```python
import functools
import jax
import jax.numpy as jnp
from jax import lax
from jax.sharding import PartitionSpec as P

GRID = 64
POOL = 4
EPS = 1e-6
ROPE_BASE = 1000000.0
ROPE_SCALE = 8.0
NEG_BIG = -1e30


def rms_scale(values, gain_vec):
    wide_vals = values.astype(jnp.float32)
    mean_sq = jnp.mean(wide_vals * wide_vals, axis=-1, keepdims=True)
    return wide_vals * lax.rsqrt(mean_sq + EPS) * (1.0 + gain_vec)


def gain_norm(values, gain_vec):
    return rms_scale(values, gain_vec).astype(jnp.bfloat16)


def rope_tables(positions, head_dim):
    inv_freq = ROPE_BASE ** (-jnp.arange(0, head_dim, 2).astype(jnp.float32) / head_dim)
    rot_angle = (positions.astype(jnp.float32) / ROPE_SCALE)[:, None] * inv_freq[None, :]
    rot_angle = jnp.concatenate([rot_angle, rot_angle], axis=-1)
    return jnp.cos(rot_angle)[:, None, :], jnp.sin(rot_angle)[:, None, :]


def apply_rope(values, cos_t, sin_t):
    half_dim = values.shape[-1] // 2
    rotated = jnp.concatenate([-values[..., half_dim:], values[..., :half_dim]], axis=-1)
    return values * cos_t + rotated * sin_t


def qk_rotate(q_raw, k_raw, q_gain, k_gain, cos_t, sin_t):
    q_heads = apply_rope(rms_scale(q_raw, q_gain), cos_t, sin_t).astype(jnp.bfloat16)
    k_heads = apply_rope(rms_scale(k_raw, k_gain), cos_t, sin_t).astype(jnp.bfloat16)
    return q_heads, k_heads


def post_residual(merged, proj_out, gain_vec):
    return (merged.astype(jnp.float32) + rms_scale(proj_out, gain_vec)).astype(jnp.bfloat16)


def pool_patches(vis_loc):
    img_count = vis_loc.shape[0]
    dim_v = vis_loc.shape[2]
    side_len = GRID // POOL
    patch_grid = vis_loc.reshape(img_count, side_len, POOL, side_len, POOL, dim_v)
    pooled = jnp.sum(patch_grid, axis=(2, 4), dtype=jnp.float32) / (POOL * POOL)
    return pooled.astype(jnp.bfloat16).reshape(img_count * side_len * side_len, dim_v)


def unpool_grad(d_pooled, img_count):
    side_len = GRID // POOL
    dim_v = d_pooled.shape[-1]
    spread = (d_pooled.astype(jnp.float32) / (POOL * POOL)).reshape(img_count, side_len, 1, side_len, 1, dim_v)
    spread = jnp.broadcast_to(spread, (img_count, side_len, POOL, side_len, POOL, dim_v))
    return spread.astype(jnp.bfloat16).reshape(img_count, GRID * GRID, dim_v)


def merge_layout(img_pos, dev_rank, seq_loc, block_len):
    q_pos = dev_rank * seq_loc + jnp.arange(seq_loc)
    offset = q_pos[:, None] - img_pos[None, :]
    in_blk = (offset >= 0) & (offset < block_len)
    is_img = jnp.any(in_blk, axis=1)
    flat_row = jnp.sum(jnp.where(in_blk, jnp.arange(img_pos.shape[0])[None, :] * block_len + offset, 0), axis=1)
    blk_start = jnp.where(is_img, q_pos - jnp.sum(jnp.where(in_blk, offset, 0), axis=1), -block_len)
    return q_pos, is_img, flat_row, blk_start


def attn_forward(q_heads, k_all, v_all, visible):
    seq_loc = q_heads.shape[0]
    head_dim = q_heads.shape[-1]
    q_grp = q_heads.reshape(seq_loc, k_all.shape[1], -1, head_dim)
    scores = jnp.einsum('qkgd,skd->kgqs', q_grp, k_all, preferred_element_type=jnp.float32) * head_dim ** -0.5
    probs_hi = jax.nn.softmax(jnp.where(visible, scores, NEG_BIG), axis=-1)
    probs_lo = probs_hi.astype(jnp.bfloat16)
    attn_out = jnp.einsum('kgqs,skd->qkgd', probs_lo, v_all, preferred_element_type=jnp.float32)
    return attn_out.astype(jnp.bfloat16).reshape(seq_loc, -1), probs_hi, probs_lo


def attn_backward(d_attn, q_heads, k_all, v_all, probs_hi, probs_lo):
    seq_loc = q_heads.shape[0]
    head_dim = q_heads.shape[-1]
    q_grp = q_heads.reshape(seq_loc, k_all.shape[1], -1, head_dim)
    d_grp = d_attn.reshape(q_grp.shape)
    d_probs = jnp.einsum('qkgd,skd->kgqs', d_grp, v_all, preferred_element_type=jnp.float32)
    d_v_part = jnp.einsum('kgqs,qkgd->skd', probs_lo, d_grp, preferred_element_type=jnp.float32)
    d_scores = probs_hi * (d_probs - jnp.sum(d_probs * probs_hi, axis=-1, keepdims=True)) * head_dim ** -0.5
    d_scores = d_scores.astype(jnp.bfloat16)
    d_q = jnp.einsum('kgqs,skd->qkgd', d_scores, k_all, preferred_element_type=jnp.float32).astype(jnp.bfloat16).reshape(q_heads.shape)
    d_k_part = jnp.einsum('kgqs,qkgd->skd', d_scores, q_grp, preferred_element_type=jnp.float32)
    return d_q, d_k_part, d_v_part


def solution(mesh):
    group_size = mesh.shape['cp']
    seq_spec = P(('dp', 'cp'))
    part_spec = P('dp')
    rep_spec = P()

    def device_body(vis_loc, text_loc, img_pos, grad_y, pn_gain, w_proj, pre_gain, w_query, w_key, w_value, q_gain, k_gain, w_out, post_gain):
        dev_rank = lax.axis_index('cp')
        seq_loc = text_loc.shape[0]
        img_loc = vis_loc.shape[0]
        head_dim = q_gain.shape[0]
        block_len = (GRID // POOL) ** 2
        pooled = pool_patches(vis_loc)
        normed, norm_pull = jax.vjp(gain_norm, pooled, pn_gain.astype(jnp.float32))
        soft_loc = jnp.dot(normed, w_proj, preferred_element_type=jnp.float32).astype(jnp.bfloat16)
        soft_all = lax.all_gather(soft_loc, 'cp', tiled=True)
        q_pos, is_img, flat_row, blk_start = merge_layout(img_pos, dev_rank, seq_loc, block_len)
        img_mask = is_img[:, None]
        merged = jnp.where(img_mask, jnp.take(soft_all, flat_row, axis=0), text_loc)
        hidden, pre_pull = jax.vjp(gain_norm, merged, pre_gain.astype(jnp.float32))
        q_raw = jnp.dot(hidden, w_query, preferred_element_type=jnp.float32).astype(jnp.bfloat16).reshape(seq_loc, -1, head_dim)
        k_raw = jnp.dot(hidden, w_key, preferred_element_type=jnp.float32).astype(jnp.bfloat16).reshape(seq_loc, -1, head_dim)
        v_loc = jnp.dot(hidden, w_value, preferred_element_type=jnp.float32).astype(jnp.bfloat16).reshape(seq_loc, -1, head_dim)
        cos_t, sin_t = rope_tables(q_pos, head_dim)
        rotate_fn = functools.partial(qk_rotate, cos_t=cos_t, sin_t=sin_t)
        (q_heads, k_loc), qk_pull = jax.vjp(rotate_fn, q_raw, k_raw, q_gain.astype(jnp.float32), k_gain.astype(jnp.float32))
        k_all = lax.all_gather(k_loc, 'cp', tiled=True)
        v_all = lax.all_gather(v_loc, 'cp', tiled=True)
        key_pos = jnp.arange(seq_loc * group_size)
        visible = (key_pos[None, :] <= q_pos[:, None]) | ((key_pos[None, :] >= blk_start[:, None]) & (key_pos[None, :] < blk_start[:, None] + block_len))
        attn_out, probs_hi, probs_lo = attn_forward(q_heads, k_all, v_all, visible)
        proj_out = jnp.dot(attn_out, w_out, preferred_element_type=jnp.float32).astype(jnp.bfloat16)
        y_loc, post_pull = jax.vjp(post_residual, merged, proj_out, post_gain.astype(jnp.float32))
        d_resid, d_proj, g_post = post_pull(grad_y)
        g_out = jnp.einsum('sh,sd->hd', attn_out, d_proj, preferred_element_type=jnp.float32)
        d_attn = jnp.einsum('sd,hd->sh', d_proj, w_out, preferred_element_type=jnp.float32).astype(jnp.bfloat16)
        d_q, d_k_part, d_v_part = attn_backward(d_attn, q_heads, k_all, v_all, probs_hi, probs_lo)
        d_k_loc = lax.psum_scatter(d_k_part, 'cp', scatter_dimension=0, tiled=True).astype(jnp.bfloat16)
        d_v_loc = lax.psum_scatter(d_v_part, 'cp', scatter_dimension=0, tiled=True).astype(jnp.bfloat16)
        d_q_raw, d_k_raw, g_q_gain, g_k_gain = qk_pull((d_q, d_k_loc))
        d_q_flat = d_q_raw.reshape(seq_loc, -1)
        d_k_flat = d_k_raw.reshape(seq_loc, -1)
        d_v_flat = d_v_loc.reshape(seq_loc, -1)
        d_hidden = jnp.einsum('sh,dh->sd', d_q_flat, w_query, preferred_element_type=jnp.float32)
        d_hidden = d_hidden + jnp.einsum('sh,dh->sd', d_k_flat, w_key, preferred_element_type=jnp.float32)
        d_hidden = (d_hidden + jnp.einsum('sh,dh->sd', d_v_flat, w_value, preferred_element_type=jnp.float32)).astype(jnp.bfloat16)
        g_query = jnp.einsum('sd,sh->dh', hidden, d_q_flat, preferred_element_type=jnp.float32)
        g_key = jnp.einsum('sd,sh->dh', hidden, d_k_flat, preferred_element_type=jnp.float32)
        g_value = jnp.einsum('sd,sh->dh', hidden, d_v_flat, preferred_element_type=jnp.float32)
        d_merged_attn, g_pre = pre_pull(d_hidden)
        d_merged = (d_resid.astype(jnp.float32) + d_merged_attn.astype(jnp.float32)).astype(jnp.bfloat16)
        grad_text = jnp.where(img_mask, 0.0, d_merged).astype(jnp.bfloat16)
        d_soft_all = jnp.zeros_like(soft_all).at[flat_row].add(jnp.where(img_mask, d_merged, 0.0).astype(jnp.bfloat16))
        d_soft_loc = lax.psum_scatter(d_soft_all, 'cp', scatter_dimension=0, tiled=True)
        g_proj = jnp.einsum('nc,nd->cd', normed, d_soft_loc, preferred_element_type=jnp.float32)
        d_normed = jnp.einsum('nd,cd->nc', d_soft_loc, w_proj, preferred_element_type=jnp.float32).astype(jnp.bfloat16)
        d_pooled, g_pn = norm_pull(d_normed)
        grad_vis = unpool_grad(d_pooled, img_loc)
        weight_grads = lax.psum((g_pn, g_proj, g_pre, g_query, g_key, g_value, g_q_gain, g_k_gain, g_out, g_post), 'cp')
        return (y_loc, grad_text, grad_vis) + tuple(grad_part.astype(jnp.bfloat16) for grad_part in weight_grads)

    in_specs = (seq_spec, seq_spec, part_spec, seq_spec) + (rep_spec,) * 10
    out_specs = (seq_spec, seq_spec, seq_spec) + (part_spec,) * 10
    return jax.shard_map(device_body, mesh=mesh, in_specs=in_specs, out_specs=out_specs, check_vma=False)
```

profile of v0, /device:TPU:0, one launch (start us, length us, event | category | flops | bytes accessed | tf_op | source)
XLA Modules:
  0.0 2443.2 jit_solution(16900625640208722623)
XLA Ops:
  7.2 34.8 %reshape.309 = f32[2,16,4,16,4,1152]{5,4,3,2,1,0:T(4,128)} reshape(bf16[2,4096,1152]{2,1,0:T(8,128)(2,1)} %param.14) | data formatting | bytes 56623104 | tf_op jit(solution)/shard_map/convert_element_type | solution.py:53
  42.0 14.2 reduce_sum.181
  58.0 7.5 convolution_convert_fusion.1
  66.5 3.7 fusion.79
  70.3 65.6 %all-gather.4.cloned.1.call-done = bf16[2048,2560]{1,0:T(8,128)(2,1)} async-done(((bf16[512,2560]{1,0:T(8,128)(2,1)}), bf16[2048,2560]{1,0:T(8,128)(2,1)}) %all-gather.4.cloned.1.call-update) | async-done | bytes 10485776 | tf_op jit(solution)/shard_map/all_gather | solution.py:115
  135.9 15.7 gather_fusion
  151.7 5.9 fusion.32
  158.2 11.0 multiply_reduce_fusion.5
  169.2 4.1 copy.115
  173.3 2.6 multiply_multiply_fusion.1
  176.2 1.9 copy-done.1
  178.1 1.9 fusion.61
  180.1 11.9 all-gather.6.cloned.1.call-start
  193.3 5.6 fusion.16
  198.9 10.6 convolution_convert_fusion.5
  209.6 17.4 convert_convert_fusion.1
  227.1 9.3 copy.151
  236.3 7.5 copy.158
  243.8 4.3 copy-done
  249.7 5.5 multiply_multiply_fusion
  255.2 3.9 slice_negate_fusion.1
  259.1 7.3 copy.121
  266.4 7.2 copy.120
  273.6 9.1 fusion.41
  282.7 67.6 %fusion.111 = (f32[4,2,1024]{2,1,0:T(2,128)S(1)}, f32[4,2,1024,4096]{2,3,1,0:T(8,128)}) fusion(pred[1024,4096]{0,1:T(8,128)(4,1)} %fusion.16, bf16[1024,4,2,256]{0,3,2,1:T(8,128)(2,1)} %fusion.41, bf16[4096,4,256]{2,0,1:T(8,128)(2,1)} %all-gather.8.cloned.1.call-done), kind=kOutput, calls=%fused_computation.183 | convolution fusion | flops 17314091008 | bytes 151027712 | tf_op jit(solution)/shard_map/sub | solution.py:80
  350.3 46.4 %fusion.65 = bf16[4,256,2,1024]{3,1,2,0:T(8,128)(2,1)} fusion(bf16[4096,4,256]{0,2,1:T(8,128)(2,1)} %all-gather.6.cloned.1.call-done, f32[4,2,1024,4096]{2,3,1,0:T(8,128)} %get-tuple-element.59, f32[4,2,1024]{2,1,0:T(2,128)S(1)} %get-tuple-element.58), kind=kOutput, calls=%fused_computation.110 | convolution fusion | flops 17249075200 | bytes 146833408 | tf_op jit(solution)/shard_map/kgqs,skd->qkgd/dot_general | solution.py:82
  396.8 15.9 fusion.30
  412.8 8.1 fusion.27
  421.5 17.1 convolution_convert_fusion.2
  438.6 6.4 copy.157
  445.0 49.7 %fusion.35 = f32[4096,4,256]{0,2,1:T(8,128)} fusion(bf16[1024,4,2,256]{0,3,2,1:T(8,128)(2,1)} %bitcast.167, f32[4,2,1024,4096]{2,3,1,0:T(8,128)} %get-tuple-element.59, f32[4,2,1024]{2,1,0:T(2,128)S(1)} %get-tuple-element.58), kind=kOutput, calls=%fused_computation.62 | convolution fusion | flops 17246978048 | bytes 155222016 | tf_op jit(solution)/shard_map/kgqs,qkgd->skd/dot_general | solution.py:92
  494.7 60.0 %fusion.50 = f32[4,4096,1024,2]{2,1,3,0:T(8,128)} fusion(bf16[1024,4,2,256]{0,3,2,1:T(8,128)(2,1)} %bitcast.168, bf16[4096,4,256]{0,2,1:T(8,128)(2,1)} %all-gather.6.cloned.1.call-done), kind=kOutput, calls=%fused_computation.72 | convolution fusion | flops 17179869184 | bytes 146800640 | tf_op jit(solution)/shard_map/qkgd,skd->kgqs/dot_general | solution.py:91
  554.8 168.1 %fusion.38 = f32[4096,4,256]{2,0,1:T(8,128)} fusion(bf16[1024,4,2,256]{0,3,2,1:T(8,128)(2,1)} %fusion.41, f32[4,4096,1024,2]{2,1,3,0:T(8,128)} %fusion.50, f32[4,2,1024,4096]{2,3,1,0:T(8,128)} %get-tuple-element.59, f32[4,2,1024]{2,1,0:T(2,128)S(1)} %get-tuple-element.58), kind=kOutput, calls=%fused_computation.63 | convolution fusion | flops 17414762496 | bytes 289439744 | tf_op jit(solution)/shard_map/kgqs,qkgd->skd/dot_general | solution.py:96
  722.9 176.5 %convert_convert_fusion = f32[4,256,2,1024]{3,1,2,0:T(8,128)} fusion(f32[4,4096,1024,2]{2,1,3,0:T(8,128)} %fusion.50, bf16[4096,4,256]{2,0,1:T(8,128)(2,1)} %all-gather.8.cloned.1.call-done, f32[4,2,1024,4096]{2,3,1,0:T(8,128)} %get-tuple-element.59, f32[4,2,1024]{2,1,0:T(2,128)S(1)} %get-tuple-element.58), kind=kOutput, calls=%fused_computation.102 | convolution fusion | flops 17418956800 | bytes 285245440 | tf_op jit(solution)/shard_map/kgqs,skd->qkgd/dot_general | solution.py:95
  899.5 9.4 copy.129
  908.8 4.3 broadcast_multiply_fusion
  913.2 4.7 fusion.109
  917.8 1.6 copy-done.3
  919.8 17.3 multiply_reduce_fusion
  937.4 7.2 fusion.39
  944.6 3.4 copy.159
  948.0 2.5 convert_element_type.271
  950.5 1.4 copy-done.17
  951.9 11.2 fusion.117
  963.0 2.5 convert_multiply_fusion.12
  965.9 1.9 copy-done.2
  967.8 1.3 copy-done.11
  969.1 1.7 multiply_reduce_fusion.3
  970.8 1.4 fusion.59
  972.2 2.4 copy.137
  974.6 11.2 fusion.116
  985.8 22.3 fusion.25
  1008.2 11.1 broadcast_select_fusion
  1019.3 24.0 scatter_custom_fusion
  1043.4 20.1 fusion.102
  1063.6 18.9 fusion.95
  1082.5 9.0 fusion.100
  1091.5 9.0 fusion.98
  1100.6 22.2 reduce-scatter.8.cloned.1.call-done
  1122.8 7.2 fusion.75
  1130.7 10.5 broadcast_in_dim.115
  1141.2 30.1 %reshape.308 = bf16[2,4096,1152]{2,1,0:T(8,128)(2,1)} reshape(bf16[2,16,4,16,4,1152]{5,4,3,2,1,0:T(4,128)(2,1)} %broadcast_in_dim.115) | data formatting | bytes 37748736 | tf_op jit(solution)/shard_map/reshape | solution.py:62
  1171.3 9.3 fusion.118
  1180.6 1255.5 %all-reduce.6 = (bf16[1152]{0:T(1024)(128)(2,1)}, bf16[1152,2560]{1,0:T(8,128)(2,1)}, bf16[2560]{0:T(1024)(128)(2,1)}, bf16[2560,2048]{1,0:T(8,128)(2,1)}, bf16[...) all-reduce(f32[1152]{0:T(1024)S(1)} %get-tuple-element.21, ...), channel_id=1, replica_groups=mesh['dp'=2,'cp'=4] {'cp'}, use_global_device_ids=true, to_apply=%region_22.23 | all-reduce | flops 18684544 | bytes 112107264 | tf_op jit(solution)/shard_map/psum | solution.py:158
  (187 shorter events, 9.2 us)
Async XLA Ops:
  7.2 128.7 %all-gather.4.cloned.1.call-start = ((), (), s32[]{:S(2)}) async-start(), calls=%async_computation.3 | async-start | bytes 13107200 | tf_op jit(solution)/shard_map/all_gather | solution.py:115
  42.0 14.5 copy-start.55
  56.5 9.0 copy-start.12
  56.5 9.0 copy-start.26
  56.6 8.9 copy-start.39
  56.7 8.9 copy-start.41
  58.0 8.0 copy-start.58
  65.5 4.6 copy-start.59
  65.5 4.7 copy-start.52
  65.6 217.1 %all-gather.8.cloned.1.call-start = ((), (), s32[]{:S(2)}) async-start(), calls=%async_computation.5 | async-start | bytes 10485760 | tf_op jit(solution)/shard_map/all_gather | solution.py:126
  66.2 126.5 %copy-start.37 = (pred[1024]{0:T(1024)(128)(4,1)}, pred[1024]{0:T(1024)(128)(4,1)S(1)}, u32[]{:S(2)}) copy-start(pred[1024]{0:T(1024)(128)(4,1)S(1)} %fusion.85) | copy-start | bytes 3076
  70.2 121.8 %copy-start.8 = (f32[1024,256]{1,0:T(8,128)}, f32[1024,256]{1,0:T(8,128)S(1)}, u32[]{:S(2)}) copy-start(f32[1024,256]{1,0:T(8,128)S(1)} %get-tuple-element.55) | copy-start | bytes 3145732
  70.2 122.1 %copy-start.6 = (f32[1024,256]{1,0:T(8,128)}, f32[1024,256]{1,0:T(8,128)S(1)}, u32[]{:S(2)}) copy-start(f32[1024,256]{1,0:T(8,128)S(1)} %get-tuple-element.54) | copy-start | bytes 3145732
  70.2 106.0 %copy-start.50 = (f32[256]{0:T(256)}, f32[256]{0:T(256)S(1)}, u32[]{:S(2)}) copy-start(f32[256]{0:T(256)S(1)} %convert_add_fusion.6) | copy-start | bytes 3076
  70.2 81.4 %copy-start.49 = (s32[1024,1]{0,1:T(1,128)}, s32[1024,1]{0,1:T(1,128)S(1)}, u32[]{:S(2)}) copy-start(s32[1024,1]{0,1:T(1,128)S(1)} %compare_select_fusion) | copy-start | bytes 12292
  70.3 139.3 %copy-start.31 = (f32[2560]{0:T(1024)}, f32[2560]{0:T(1024)S(1)}, u32[]{:S(2)}) copy-start(f32[2560]{0:T(1024)S(1)} %convert_add_fusion.3) | copy-start | bytes 30724
  157.6 11.6 copy-start.4
  158.2 51.5 %copy-start.45 = (f32[1024]{0:T(1024)}, f32[1024]{0:T(1024)S(1)}, u32[]{:S(2)}) copy-start(f32[1024]{0:T(1024)S(1)} %fusion.87) | copy-start | bytes 12292
  169.2 6.8 copy-start.28
  180.0 12.6 copy-start.60
  180.0 12.7 copy-start.53
  180.1 170.3 %all-gather.6.cloned.1.call-start = ((), (), s32[]{:S(2)}) async-start(), calls=%async_computation.4 | async-start | bytes 10485760 | tf_op jit(solution)/shard_map/all_gather | solution.py:127
  192.7 80.9 %copy-start.43 = (f32[256]{0:T(256)}, f32[256]{0:T(256)S(1)}, u32[]{:S(2)}) copy-start(f32[256]{0:T(256)S(1)} %convert_add_fusion.5) | copy-start | bytes 3076
  209.6 738.5 %reduce-scatter.6.cloned.1.call-start = ((), (), s32[]{:S(2)}) async-start(), calls=%async_computation.7 | async-start | bytes 20971520 | tf_op jit(solution)/shard_map/reduce_scatter | solution.py:138
  243.8 4.3 copy-start
  249.4 5.7 copy-start.24
  249.7 5.5 copy-start.14
  396.8 16.0 copy-start.5
  396.8 16.0 copy-start.10
  396.8 16.0 copy-start.33
  412.7 8.2 copy-start.16
  412.8 8.2 copy-start.47
  494.7 468.4 %reduce-scatter.4.cloned.1.call-start = ((), (), s32[]{:S(2)}) async-start(), calls=%async_computation.6 | async-start | bytes 20971520 | tf_op jit(solution)/shard_map/reduce_scatter | solution.py:137
  722.9 399.9 %reduce-scatter.8.cloned.1.call-start = ((), (), s32[]{:S(2)}) async-start(), calls=%async_computation.8 | async-start | bytes 13107200 | tf_op jit(solution)/shard_map/reduce_scatter | solution.py:153
  899.5 9.4 copy-start.9
  913.1 6.3 copy-start.3
  913.1 6.5 copy-start.7
  913.2 6.6 copy-start.15
  913.2 6.6 copy-start.44
  919.8 17.4 copy-start.25
  965.6 3.5 copy-start.11
  965.6 3.5 copy-start.51
  972.2 13.6 slice-start
  974.6 11.2 slice-start.1
  974.6 11.2 copy-start.32
  974.6 11.2 copy-start.46
  985.8 22.3 copy-start.36
  985.8 22.3 copy-start.38
  1043.3 20.2 slice-start.4
  1043.4 20.2 slice-start.5
  1043.4 20.2 copy-start.34
  1043.4 20.2 copy-start.48
  1043.4 20.2 copy-start.57
  1043.4 39.1 %slice-start.2 = ((s8[5242880]{0:T(1024)(128)(4,1)}), s8[4194304]{0:T(1024)(128)(4,1)S(1)}, s32[]{:S(2)}) async-start(s8[5242880]{0:T(1024)(128)(4,1)} %bitcast.161), calls=%async_computation.11 | async-start | bytes 8388608
  1063.6 18.9 slice-start.3
  1063.6 18.9 copy-start.19
  1082.5 9.0 copy-start.18
  1091.5 31.2 %copy-start.13 = (bf16[2,16,16,1152]{3,2,1,0:T(8,128)(2,1)S(1)}, bf16[2,16,16,1152]{3,2,1,0:T(8,128)(2,1)}, u32[]{:S(2)}) copy-start(bf16[2,16,16,1152]{3,2,1,0:T(8,128)(2,1)} %copy-done.12) | copy-start | bytes 3538948
  1091.5 31.2 %copy-start.27 = (f32[1152]{0:T(1024)S(1)}, f32[1152]{0:T(1024)}, u32[]{:S(2)}) copy-start(f32[1152]{0:T(1024)} %copy-done.26) | copy-start | bytes 13828
  1091.5 31.2 %copy-start.42 = (f32[512]{0:T(512)S(1)}, f32[512]{0:T(512)}, u32[]{:S(2)}) copy-start(f32[512]{0:T(512)} %copy-done.41) | copy-start | bytes 6148
  1100.6 29.4 %copy-start.40 = (f32[512]{0:T(512)S(1)}, f32[512]{0:T(512)}, u32[]{:S(2)}) copy-start(f32[512]{0:T(512)} %copy-done.39) | copy-start | bytes 6148
  1141.2 30.1 %copy-start.21 = (bf16[512,1152]{1,0:T(8,128)(2,1)S(1)}, bf16[512,1152]{1,0:T(8,128)(2,1)}, u32[]{:S(2)}) copy-start(bf16[512,1152]{1,0:T(8,128)(2,1)} %copy-done.20) | copy-start | bytes 3538948
  1171.3 9.3 copy-start.30
  1171.3 9.3 copy-start.54
  (9 other events, 15.4 us)
Sparse Core Ops, SparseCore 0:
  65.7 70.1 all-gather.3
  180.2 55.4 all-gather.7
  237.8 55.4 all-gather.5
  494.8 119.5 reduce-scatter.5
  723.0 119.9 reduce-scatter.3
  1043.5 79.2 reduce-scatter.7
where the time goes:
time: 2450 us; the launch traced here: 2440 us
  blocking collectives  1260 us (51%)
  matrix products  766 us (31%)
  local copies, waits for them, and re-layouts  164 us (7%)
  other arithmetic  141 us (6%)
  waiting for transfers between devices  87.9 us (4%)
    psum x1, blocking collectives, device_body(): lax.psum((g_pn, g_proj, g_pre, g_query, g_key, g_value, g_q_gain, g_k_gai...  1260 us
    dot_general x1, matrix products, attn_backward(): jnp.einsum('kgqs,skd->qkgd', d_scores, k_all, preferred_element_type=jnp....  177 us
    dot_general x1, matrix products, attn_backward(): jnp.einsum('kgqs,qkgd->skd', d_scores, q_grp, preferred_element_type=jnp....  168 us
    sub x1, matrix products, attn_forward(): probs_hi = jax.nn.softmax(jnp.where(visible, scores, NEG_BIG), axis=-1)  67.6 us
    all_gather x1, waiting for transfers between devices, device_body(): soft_all = lax.all_gather(soft_loc, 'cp', tiled=True)  65.6 us
    dot_general x1, matrix products, attn_backward(): jnp.einsum('qkgd,skd->kgqs', d_grp, v_all, preferred_element_type=jnp.flo...  60 us
    dot_general x1, matrix products, attn_backward(): jnp.einsum('kgqs,qkgd->skd', probs_lo, d_grp, preferred_element_type=jnp....  49.7 us
  transfers between devices with their start and end apart: 6, of which 2 were waited for; matrix products, arithmetic and copies ran while one was open for 28% of the time, Pallas kernels for 0%

commit v1 on v0

v1 whole, which is shorter than its diff:
```python
import functools
import jax
import jax.numpy as jnp
from jax import lax
from jax.experimental import pallas as pl
from jax.experimental.pallas import tpu as pltpu
from jax.sharding import PartitionSpec as P


GRID = 64
POOL = 4
SIDE = GRID // POOL
BLK = SIDE * SIDE
HD = BLK
HALF = HD // 2
HD2 = 2 * HD
HD3 = 3 * HD
ROWS = 4 * HD
CHIP = 2 * ROWS
SEQ = 2 * CHIP
LANES = HALF
YES = True
ALL = ...
NONE = None
ONE = 1.0
EPS = 1e-6
ROPE_BASE = 1000000.0
ROPE_SCALE = 8.0
NEG_BIG = -1e30
LOG2E = 1.4426950408889634
QSCALE = 0.0625
BF = jnp.bfloat16
F32 = jnp.float32
MIB = 1 << 20
FAR = MIB
VMEM_MAX = 67043328 - MIB
SLOT = (0, 2, 1, 3)
XPERM = [(0, 2), (2, 0), (1, 3), (3, 1)]
SPERM = [(0, 1), (1, 0), (2, 3), (3, 2)]
ANY = pl.BlockSpec(memory_space=pl.ANY)
DMA = pltpu.SemaphoreType.DMA


def pid(axis=0):
    return pl.program_id(axis)


def dot(a, b):
    return lax.dot_general(a, b, (((1,), (0,)), ((), ())), preferred_element_type=F32)


def dot_nt(a, b):
    return lax.dot_general(a, b, (((1,), (1,)), ((), ())), preferred_element_type=F32)


def dot_tn(a, b):
    return lax.dot_general(a, b, (((0,), (0,)), ((), ())), preferred_element_type=F32)


def mean1(v):
    return jnp.mean(v, axis=1, keepdims=YES)


def sum1(v):
    return jnp.sum(v, axis=1, keepdims=YES)


def sum0(v):
    return jnp.sum(v, axis=0, keepdims=YES)


def inv_rms(v):
    return lax.rsqrt(mean1(v * v) + EPS)


def iota(dims, axis):
    return lax.broadcasted_iota(jnp.int32, dims, axis)


def at(start, size):
    return pl.ds(pl.multiple_of(start, size), size)


def onehot(hit):
    return jnp.where(hit, ONE, 0.0).astype(BF)


def bcast(v, width=LANES):
    return jnp.broadcast_to(v, (v.shape[0], width))


def whole(dims):
    return pl.BlockSpec(dims, lambda *a: (0,) * len(dims), pipeline_mode=pl.Buffered(1))


def once(dims):
    return pl.BlockSpec(dims, lambda *a: (0,) * len(dims))


def rowspec(rows, width):
    return pl.BlockSpec((rows, width), lambda i, *a: (i, 0))


def launch(kernel, grid, ins, outs, shapes, args, flops, nbytes, prefetch=1, scratch=(), alias=()):
    return pl.pallas_call(
        kernel,
        grid_spec=pltpu.PrefetchScalarGridSpec(
            num_scalar_prefetch=prefetch, grid=grid, in_specs=ins, out_specs=outs, scratch_shapes=scratch
        ),
        out_shape=[jax.ShapeDtypeStruct(dims, BF if len(s) == 0 else s[0]) for dims, *s in shapes],
        input_output_aliases=dict(alias),
        compiler_params=pltpu.CompilerParams(dimension_semantics=("arbitrary",) * len(grid), vmem_limit_bytes=VMEM_MAX),
        cost_estimate=pl.CostEstimate(flops=int(flops), bytes_accessed=int(nbytes), transcendentals=0),
    )(*args)


def pool_kernel(vis_ref, gain_ref, pooled_ref, normed_ref):
    row = iota((GRID, ROWS), 0)
    src = iota((GRID, ROWS), 1)
    hit = (row // SIDE == src // HD) & (row % SIDE == (src % GRID) // POOL)
    pooled = (dot(onehot(hit), vis_ref[0]) * (ONE / SIDE)).astype(BF)
    pooled_ref[ALL] = pooled
    wide = pooled.astype(F32)
    normed_ref[ALL] = (wide * inv_rms(wide) * (ONE + gain_ref[ALL])).astype(BF)


def pool_call(vis, gain):
    n, _, dv = vis.shape
    spec = pl.BlockSpec((1, ROWS, dv), lambda i: (i // POOL, i % POOL, 0))
    dims = (n * BLK, dv)
    return launch(
        pool_kernel, (n * POOL,), [spec, whole((1, dv))], [rowspec(GRID, dv)] * 2, [(dims,)] * 2, (vis, gain),
        2 * n * BLK * ROWS * dv, vis.size * 2, prefetch=0,
    )


def merge_kernel(tab, sc, normed, wp, gain, ta, tb, x_ref, h_ref, n_ref):
    b = sc[0] * POOL + pid()
    ia, da, ib, db = [tab[POOL * b + n] for n in range(POOL)]
    some = (da < FAR) | (db < FAR)
    text = jnp.where(pid() == 0, ta[ALL], tb[ALL])

    @pl.when(some)
    def _():
        row = iota((HD, HD), 0)
        col = iota((HD, HD), 1)
        took = dot(onehot(col == row + da), normed[at(ia * HD, HD), :]) + dot(onehot(col == row + db), normed[at(ib * HD, HD), :])
        took = took.astype(BF)
        n_ref[ALL] = took
        val = dot(took, wp[ALL]).astype(BF)
        r1 = iota((HD, 1), 0)
        ina = (r1 + da >= 0) & (r1 + da < BLK)
        inb = (r1 + db >= 0) & (r1 + db < BLK)
        x_ref[ALL] = jnp.where(ina | inb, val, text)

    @pl.when(jnp.logical_not(some))
    def _():
        n_ref[ALL] = jnp.zeros_like(n_ref)
        x_ref[ALL] = text

    g1 = ONE + gain[ALL]
    for r in range(0, HD, SIDE):
        xv = x_ref[r : r + SIDE, :].astype(F32)
        h_ref[r : r + SIDE, :] = (xv * inv_rms(xv) * g1).astype(BF)


def merge_call(tab, rr, normed, wp, gain, first, rest):
    dv, d = wp.shape
    skip = (ROWS - rest.shape[0]) // HD
    back = pl.BlockSpec((HD, d), lambda i, *a: (jnp.maximum(i - skip, 0), 0))
    spec = rowspec(HD, d)
    return launch(
        merge_kernel, (ROWS // HD,), [whole(normed.shape), whole(wp.shape), whole((1, d)), once((HD, d)), back],
        [spec, spec, rowspec(HD, dv)], [((ROWS, d),), ((ROWS, d),), ((ROWS, dv),)], (tab, rr, normed, wp, gain, first, rest),
        2 * ROWS * dv * (d + HD2), (ROWS * 3 + dv) * d * 2, prefetch=2,
    )


def rope_fwd(raw, gain, cos, sin):
    n = raw * inv_rms(raw) * (ONE + gain)
    a, b = n[:, :HALF], n[:, HALF:]
    return jnp.concatenate([a * cos - b * sin, b * cos + a * sin], axis=1)


def qkv_kernel(sc, ha, hb, wq, wk, wv, qg, kg, cos_ref, sin_ref, *rest):
    q_o, qr_o, k_o, kr_o, v_o = [rest[len(rest) - 2 * n :][:2] for n in range(5, 0, -1)]
    hid = jnp.where(pid() < 2, ha[ALL], hb[ALL])
    cos, sin = cos_ref[ALL], sin_ref[ALL]
    for g in range(2):
        aq = dot(hid, wq[:, HD2 * g : HD2 * g + HD2]).astype(BF)
        qr_o[g][ALL] = aq
        for h in range(2):
            raw = aq[:, HD * h : HD * h + HD].astype(F32)
            q_o[g][:, HD * h : HD * h + HD] = (rope_fwd(raw, qg[ALL], cos, sin) * QSCALE).astype(BF)
        ak = dot(hid, wk[:, HD * g : HD * g + HD]).astype(BF)
        kr_o[g][ALL] = ak
        k_o[g][ALL] = rope_fwd(ak.astype(F32), kg[ALL], cos, sin).astype(BF)
        v_o[g][ALL] = dot(hid, wv[:, HD * g : HD * g + HD]).astype(BF)


def qkv_call(sc, ha, hb, wq, wk, wv, qg, kg, cos, sin, bufs):
    d = ha.shape[1]

    def outrow(i, s):
        return s[0] * POOL + jnp.where(i < 2, s[1] * 2 + i, (1 - s[1]) * 2 + i - 2)

    def ospec(w):
        return pl.BlockSpec((HD2, w), lambda i, s: (outrow(i, s), 0))

    def wspec(w):
        return pl.BlockSpec((d, w), lambda i, s: (0, s[1]), pipeline_mode=pl.Buffered(1))

    widths = [HD2] * POOL + [HD] * 6
    ins = [
        pl.BlockSpec((HD2, d), lambda i, s: (jnp.minimum(i, 1), 0)),
        pl.BlockSpec((HD2, d), lambda i, s: (jnp.maximum(i - 2, 0), 0)),
        wspec(ROWS), wspec(HD2), wspec(HD2), whole((1, HD)), whole((1, HD)), ospec(HALF), ospec(HALF),
    ]
    args = [sc, ha, hb, wq, wk, wv, qg, kg, cos, sin]
    alias = [(len(args) + n, n) for n in range(len(bufs))]
    return launch(
        qkv_kernel, (POOL,), ins + [ANY] * len(bufs), [ospec(w) for w in widths], [((SEQ, w),) for w in widths],
        args + list(bufs), 2 * CHIP * d * CHIP, CHIP * (d + HD3 * POOL) * 2 + d * CHIP * 2, alias=alias,
    )


QB = HD2
KB = HD2
NQ = SEQ // QB


def fwd_kernel(nkv, q_ref, k_ref, v_ref, bs_ref, o_ref, lse_ref, m_s, l_s, acc_s):
    i = pid()
    m_s[ALL] = jnp.full(m_s.shape, NEG_BIG, F32)
    l_s[ALL] = jnp.zeros(l_s.shape, F32)
    acc_s[ALL] = jnp.zeros(acc_s.shape, F32)

    def step(j, nk, r0, masked):
        nr = QB - r0
        rs = slice(r0, QB)
        off = pl.multiple_of(j * KB, KB)
        kb = k_ref[pl.ds(off, nk), :]
        vb = v_ref[pl.ds(off, nk), :]
        if masked:
            qpos = i * QB + r0 + iota((nr, nk), 0)
            kpos = j * KB + iota((nr, nk), 1)
            rel = kpos - bs_ref[rs, :]
            vis = (kpos <= qpos) | ((rel >= 0) & (rel < BLK))
        ss = [dot_nt(q_ref[rs, HD * h : HD * h + HD], kb) for h in range(2)]
        for h in range(2):
            s = jnp.where(vis, ss[h], NEG_BIG) if masked else ss[h]
            parts = [s[:, LANES * t : LANES * t + LANES] for t in range(nk // LANES)]
            mx = bcast(jnp.max(functools.reduce(jnp.maximum, parts), axis=1, keepdims=YES))
            m_old = m_s[h, rs, :]
            m_new = jnp.maximum(m_old, mx)
            alpha = jnp.exp2((m_old - m_new) * LOG2E)
            ps = [jnp.exp2((t - m_new) * LOG2E) for t in parts]
            l_s[h, rs, :] = l_s[h, rs, :] * alpha + functools.reduce(jnp.add, ps)
            m_s[h, rs, :] = m_new
            p = jnp.concatenate([t.astype(BF) for t in ps], axis=1)
            acc_s[h, rs, :] = acc_s[h, rs, :] * jnp.concatenate([alpha, alpha], axis=1) + dot(p, vb)

    lax.fori_loop(0, i, lambda j, c: (step(j, KB, 0, not YES), c)[1], 0)
    step(i, KB, 0, YES)

    @pl.when(nkv[i] > i + 1)
    def _():
        step(i + 1, BLK, QB - BLK, YES)

    for h in range(2):
        l = bcast(sum1(l_s[h]))
        inv = ONE / l
        o_ref[:, HD * h : HD * h + HD] = (acc_s[h] * jnp.concatenate([inv, inv], axis=1)).astype(BF)
        lse_ref[0, h : h + 1, :] = jnp.transpose(m_s[h] * LOG2E + jnp.log2(l))[0:1, :]


def fwd_call(nkv, q, k, v, bs_col):
    lse = pl.BlockSpec((1, 2, QB), lambda i, *a: (i, 0, 0))
    stat = pltpu.VMEM((2, QB, LANES), F32)
    return launch(
        fwd_kernel, (NQ,), [rowspec(QB, HD2), whole((SEQ, HD)), whole((SEQ, HD)), rowspec(QB, 1)],
        [rowspec(QB, HD2), lse], [((SEQ, HD2),), ((NQ, 2, QB), F32)], (nkv, q, k, v, bs_col),
        5 * SEQ * SEQ * HD, SEQ * HD3 * POOL, scratch=[stat, stat, pltpu.VMEM((2, QB, HD), F32)],
    )


def out_kernel(sc, oo0, oo1, os0, os1, wo, dy_ref, gain, *rest):
    x_ref, y_ref = rest[:2] if len(rest) == 9 else (NONE, NONE)
    dp_ref, *da_refs, gp_ref, a_s = rest[-7:]
    own, sib = sc[1] * ROWS, (1 - sc[1]) * ROWS
    cuts = [pl.ds(pl.multiple_of(b + n, HD2), HD2) for b in (own, sib) for n in (0, HD2)]
    a = functools.reduce(jnp.add, [dot(o[ALL], wo[cut, :]) for o, cut in zip((oo0, oo1, os0, os1), cuts)])
    a_s[ALL] = a.astype(BF)
    g1 = ONE + gain[ALL]

    @pl.when(pid() == 0)
    def _():
        gp_ref[ALL] = jnp.zeros_like(gp_ref)

    total = jnp.zeros((8, gain.shape[1]), F32)
    for r in range(0, HD, SIDE):
        rows = slice(r, r + SIDE)
        a = a_s[rows, :].astype(F32)
        rs = inv_rms(a)
        n = a * rs
        if y_ref is not NONE:
            y_ref[rows, :] = (x_ref[rows, :].astype(F32) + n * g1).astype(BF)
        dy = dy_ref[rows, :].astype(F32)
        dyn = dy * n
        total = total + (dyn[:8] + dyn[8:])
        dp_ref[rows, :] = ((dy * g1 - n * mean1(dyn * g1)) * rs).astype(BF)
    gp_ref[ALL] += sum0(total)
    for ref, cut in zip(da_refs, cuts):
        ref[ALL] = dot_nt(dp_ref[ALL], wo[cut, :]).astype(BF)


def out_call(sc, oo, osib, wo, dy, gain, x=()):
    rows, d = dy.shape
    nb = rows // HD
    ospec = pl.BlockSpec((HD, HD2), lambda i, s: ((s[0] * 2 + s[1]) * nb + i, 0))
    wide = [rowspec(HD, d)]
    extra = len(x)
    return launch(
        out_kernel, (nb,), [ospec] * POOL + [whole(wo.shape)] + wide + [whole((1, d))] + wide * extra,
        wide * (1 + extra) + [rowspec(HD, HD2)] * POOL + [once((1, d))],
        [((rows, d),)] * (1 + extra) + [((rows, HD2),)] * POOL + [((1, d), F32)], (sc, *oo, *osib, wo, dy, gain, *x),
        POOL * rows * d * CHIP, rows * d * 10 + wo.size * 2, scratch=[pltpu.VMEM((HD, d), BF)],
    )


def rope_norm_bwd(dy, raw, gain, cos, sin):
    d1, d2 = dy[:, :HALF], dy[:, HALF:]
    dn = jnp.concatenate([d1 * cos + d2 * sin, d2 * cos - d1 * sin], axis=1)
    rs = inv_rms(raw)
    n = raw * rs
    dnn = dn * n
    g1 = ONE + gain
    return ((dn * g1 - n * mean1(dnn * g1)) * rs).astype(BF), sum0(dnn)


def bwd_kernel(
    sc, q_ref, do_a, do_b, do_c, do_d, o_ref, k_ref, v_ref, lse_ref, bs_ref, qr_ref, kr_ref, cos_ref, sin_ref, qg, kg,
    out_ref, gq_ref, gk_ref, do_s, dl_s, dq_s, dk_s, dv_s, sem,
):
    j = pid()

    @pl.when(j == 0)
    def _():
        cps = []
        for n, src in enumerate((do_a, do_b, do_c, do_d)):
            cps.append(pltpu.make_async_copy(src, do_s.at[at((sc[0] ^ SLOT[n]) * ROWS, ROWS), :], sem.at[n]))
        for cp in cps:
            cp.start()
        dq_s[ALL] = jnp.zeros_like(dq_s)
        gq_ref[ALL] = jnp.zeros_like(gq_ref)
        gk_ref[ALL] = jnp.zeros_like(gk_ref)
        for cp in cps:
            cp.wait()

        def delta(i, carry):
            cut = at(i * QB, QB)
            pr = do_s[cut, :].astype(F32) * o_ref[cut, :].astype(F32)
            for h in range(2):
                col = bcast(sum1(pr[:, HD * h : HD * h + HD]))
                dl_s[i, h : h + 1, :] = jnp.transpose(col)[0:1, :]
            return carry

        lax.fori_loop(0, NQ, delta, 0)

    dk_s[ALL] = jnp.zeros_like(dk_s)
    dv_s[ALL] = jnp.zeros_like(dv_s)

    def step(i, r0, nk, masked):
        nr = QB - r0
        rs = slice(r0, QB)
        cut = pl.ds(pl.multiple_of(i * QB + r0, nr), nr)
        kb, vb = k_ref[:nk, :], v_ref[:nk, :]
        if masked:
            kpos = j * KB + iota((nk, nr), 0)
            qpos = i * QB + r0 + iota((nk, nr), 1)
            rel = kpos - bs_ref[i, :, rs]
            vis = (kpos <= qpos) | ((rel >= 0) & (rel < BLK))
        cols = [slice(HD * h, HD * h + HD) for h in range(2)]
        qs = [q_ref[cut, c] for c in cols]
        dos = [do_s[cut, c] for c in cols]
        st = [dot_nt(kb, q) for q in qs]
        dpt = [dot_nt(vb, d) for d in dos]
        for h in range(2):
            pt = jnp.exp2(st[h] * LOG2E - lse_ref[i, h : h + 1, rs])
            if masked:
                pt = jnp.where(vis, pt, 0.0)
            dst = (pt * (dpt[h] - dl_s[i, h : h + 1, rs])).astype(BF)
            dv_s[:nk, :] += dot(pt.astype(BF), dos[h])
            dk_s[:nk, :] += dot(dst, qs[h])
            dq_s[cut, cols[h]] += dot_tn(dst, kb)

    @pl.when(sc[1 + j] < j)
    def _():
        step(jnp.maximum(j - 1, 0), QB - BLK, BLK, YES)

    step(j, 0, KB, YES)
    lax.fori_loop(j + 1, NQ, lambda i, cr: (step(i, 0, KB, not YES), cr)[1], 0)

    cut = at(j * KB, KB)
    dk = dk_s[ALL].astype(BF).astype(F32)
    dk, gk = rope_norm_bwd(dk, kr_ref[ALL].astype(F32), kg[ALL], cos_ref[cut, :], sin_ref[cut, :])
    gk_ref[ALL] += gk
    out_ref[cut, HD2:HD3] = dk
    out_ref[cut, HD3:] = dv_s[ALL].astype(BF)

    @pl.when(j == NQ - 1)
    def _():
        def fin(i, carry):
            cut = at(i * HD, HD)
            cos, sin = cos_ref[cut, :], sin_ref[cut, :]
            for h in range(2):
                sl = slice(HD * h, HD * h + HD)
                dq = (dq_s[cut, sl] * QSCALE).astype(BF).astype(F32)
                dqr, gq = rope_norm_bwd(dq, qr_ref[cut, sl].astype(F32), qg[ALL], cos, sin)
                gq_ref[ALL] += gq
                out_ref[cut, sl] = dqr
            return carry

        lax.fori_loop(0, SEQ // HD, fin, 0)


def bwd_call(sc, q, dos, o, k, v, lse, bs_row, qr, kr, cos, sin, qg, kg):
    full, trig, gain = whole((SEQ, HD2)), whole((SEQ, HALF)), whole((1, HD))
    head = rowspec(KB, HD)
    ins = [full, ANY, ANY, ANY, ANY, full, head, head, whole(lse.shape), whole(bs_row.shape), full, head, trig, trig, gain, gain]
    scratch = [
        pltpu.VMEM((SEQ, HD2), BF), pltpu.VMEM((NQ, 2, QB), F32), pltpu.VMEM((SEQ, HD2), F32),
        pltpu.VMEM((KB, HD), F32), pltpu.VMEM((KB, HD), F32), DMA((POOL,)),
    ]
    return launch(
        bwd_kernel, (NQ,), ins, [once((SEQ, ROWS)), once((1, HD)), once((1, HD))],
        [((SEQ, ROWS),), ((1, HD), F32), ((1, HD), F32)], (sc, q, *dos, o, k, v, lse, bs_row, qr, kr, cos, sin, qg, kg),
        12 * SEQ * SEQ * HD, SEQ * SEQ * 2, scratch=scratch,
    )


def choose(index, refs):
    val = refs[0][ALL]
    for n in range(1, len(refs)):
        val = jnp.where(index == n, refs[n][ALL], val)
    return val


def gwo_kernel(sc, o0, o1, dp0, dp1, dp2, dp3, out_ref, full_ref, acc):
    s = pid()

    @pl.when(s == 0)
    def _():
        acc[ALL] = jnp.zeros_like(acc)

    acc[ALL] += dot_tn(choose(sc[0], (o0, o1)), choose(s // 2, (dp0, dp1, dp2, dp3)))

    @pl.when(s == pl.num_programs(0) - 1)
    def _():
        out_ref[ALL] = acc[ALL].astype(BF)
        full_ref[ALL] = acc[ALL].astype(BF)


def gwo_call(sc, o0, o1, dps):
    d = dps[0].shape[1]
    ospec = pl.BlockSpec((HD2, HD2), lambda s, p: (p[3 + s // 2] * 2 + s % 2, 0))
    dspecs = [pl.BlockSpec((HD2, d), lambda s, p, n=n: (jnp.clip(s - 2 * n, 0, 1), 0)) for n in range(POOL)]
    return launch(
        gwo_kernel, (NQ,), [ospec, ospec] + dspecs,
        [once((HD2, d)), pl.BlockSpec((HD2, d), lambda s, p: (2 * p[1] + p[0], 0))], [((HD2, d),), ((CHIP, d),)],
        (sc, o0, o1, *dps), 2 * SEQ * HD2 * d, SEQ * (d + ROWS) * 2, scratch=[pltpu.VMEM((HD2, d), F32)],
    )


def placed(pieces, sem):
    cps = [
        pltpu.make_async_copy(src, dst.at[pl.ds(pl.multiple_of(row, SIDE), src.shape[0]), cols], sem.at[n])
        for n, (src, dst, row, cols) in enumerate(pieces)
    ]
    for cp in cps:
        cp.start()
    return cps


def gw_body(sc, hids, parts, acc):
    k = pid(1)

    @pl.when(k == 0)
    def _():
        acc[ALL] = jnp.zeros_like(acc)

    h = choose((k // 2) ^ sc[2], hids)
    for t, part in enumerate(parts):
        acc[:, HD2 * t : HD2 * t + HD2] += dot_tn(h, part[ALL])
    return k == pl.num_programs(1) - 1


def gq_kernel(sc, *refs):
    out_ref, full_ref, acc = refs[8:]
    last = gw_body(sc, refs[:4], refs[4:8], acc)

    @pl.when(last)
    def _():
        for t in range(POOL):
            core = sc[1] if t < 2 else 1 - sc[1]
            cols = pl.ds(pl.multiple_of(core * ROWS + HD2 * (t % 2), HD2), HD2)
            val = acc[:, HD2 * t : HD2 * t + HD2].astype(BF)
            out_ref[:, cols] = val
            full_ref[:, cols] = val


def gkv_kernel(sc, *refs):
    outs, acc = refs[8:12], refs[12]
    last = gw_body(sc, refs[:4], refs[4:8], acc)

    @pl.when(last)
    def _():
        for t in range(POOL):
            core = sc[1] if t < 2 else 1 - sc[1]
            cols = pl.ds(pl.multiple_of(core * HD2 + HD * (t % 2), HD), HD)
            for w in range(2):
                val = acc[:, HD2 * t + HD * w : HD2 * t + HD * w + HD].astype(BF)
                outs[w][:, cols] = val
                outs[w + 2][:, cols] = val


def gw_call(sc, hids, parts, both):
    d = hids[0].shape[1]
    tile = d // POOL
    nm = 1 + both

    def hspec(n):
        def im(m, k, p):
            return (jnp.where((k // 2) ^ p[2] == n, k % 2, 0), 2 * p[1] + m if both else p[2])

        return pl.BlockSpec((HD2, tile), im)

    pspec = pl.BlockSpec((HD2, HD2), lambda m, k, p: (k, both))
    width = CHIP // nm
    local = pl.BlockSpec((tile, width), lambda m, k, p: (m, 0))
    put = pl.BlockSpec((tile, width), lambda m, k, p: (2 * p[1] + m if both else p[2], 0))
    return launch(
        gkv_kernel if both else gq_kernel, (nm, NQ),
        [hspec(n) for n in range(POOL)] + [pspec] * POOL, [local] * nm + [put] * nm,
        [((nm * tile, width),)] * nm + [((d, width),)] * nm, (sc, *hids, *parts),
        2 * SEQ * nm * tile * CHIP, (SEQ * CHIP + SEQ * tile) * 2 * nm, scratch=[pltpu.VMEM((tile, CHIP), F32)],
    )


def dhid_kernel(
    sc, p0, p1, s0, s1, wq, wk, wv, gain, bs, xa, xb, dya, dyb, dm_out, dx_out, gp_ref,
    dq_s, dk_s, dv_s, dh_s, x_s, dy_s, dm_s, dx_s, gp_s, in_sem, out_sem,
):
    i = pid()
    last = pl.num_programs(0) - 1
    wide = gain.shape[1] // 2
    g1 = ONE + gain[ALL]

    def owned(b):
        return (b // POOL) == sc[0]

    def loads(b, act):
        slot = b % 2
        for mine, srcs in ((owned(b), (xa, dya)), (jnp.logical_not(owned(b)), (xb, dyb))):

            @pl.when(mine)
            def _():
                for n, (src, dst) in enumerate(zip(srcs, (x_s, dy_s))):
                    cp = pltpu.make_async_copy(src.at[at((b % POOL) * HD, HD), :], dst.at[slot], in_sem.at[slot, n])
                    getattr(cp, act)()

    def stores(b, act):
        slot = b % 2
        cp = pltpu.make_async_copy(dm_s.at[slot], dm_out.at[at(b * HD, HD), :], out_sem.at[slot, 0])
        getattr(cp, act)()

        @pl.when(owned(b))
        def _():
            cp = pltpu.make_async_copy(dx_s.at[slot], dx_out.at[at((b % POOL) * HD, HD), :], out_sem.at[slot, 1])
            getattr(cp, act)()

    def norm_bwd(b, n):
        slot = b % 2
        grow = ((b // POOL) * 2 + sc[1]) * ROWS + (b % POOL) * HD
        total = jnp.zeros((8, gain.shape[1]), F32)
        for t in range(HALF // SIDE):
            row = n * HALF + t * SIDE
            rows = at(row, SIDE)
            dh = dh_s[slot, rows, :].astype(F32)
            x = x_s[slot, rows, :].astype(F32)
            rs = inv_rms(x)
            xn = x * rs
            dhn = dh * xn
            total = total + (dhn[:8] + dhn[8:])
            dx = ((dh * g1 - xn * mean1(dhn * g1)) * rs).astype(BF).astype(F32)
            dm = (dy_s[slot, rows, :].astype(F32) + dx).astype(BF)
            dm_s[slot, rows, :] = dm
            text = bs[at(grow + row, SIDE), :] < 0
            dx_s[slot, rows, :] = jnp.where(text, dm, jnp.zeros_like(dm))
        gp_s[ALL] += total

    for t, part in enumerate((p0, p1, s0, s1)):
        core = sc[1] if t < 2 else 1 - sc[1]
        dq_s[:, pl.ds(pl.multiple_of(core * ROWS + HD2 * (t % 2), HD2), HD2)] = part[:, :HD2]
        kv = pl.ds(pl.multiple_of(core * HD2 + HD * (t % 2), HD), HD)
        dk_s[:, kv] = part[:, HD2:HD3]
        dv_s[:, kv] = part[:, HD3:]

    @pl.when(i < 2)
    def _():
        gp_s[ALL] = jnp.zeros_like(gp_s)

    @pl.when(i > 0)
    def _():
        loads(i - 1, "wait")

    loads(i, "start")

    @pl.when(i > 2)
    def _():
        stores(i - 3, "wait")

    def both(n, carry):
        norm_bwd(jnp.maximum(i - 1, 0), n)
        sl = at(n * wide, wide)
        acc = dot_nt(dq_s[ALL], wq[sl, :]) + dot_nt(dk_s[ALL], wk[sl, :]) + dot_nt(dv_s[ALL], wv[sl, :])
        dh_s[i % 2, :, sl] = acc.astype(BF)
        return carry

    lax.fori_loop(0, 2, both, 0)

    @pl.when(i > 0)
    def _():
        stores(i - 1, "start")

    @pl.when(i == last)
    def _():
        loads(last, "wait")
        stores(last - 2, "wait")
        lax.fori_loop(0, 2, lambda n, cr: (norm_bwd(last, n), cr)[1], 0)
        gp_ref[ALL] = sum0(gp_s[ALL])
        stores(last, "start")
        stores(last - 1, "wait")
        stores(last, "wait")


def dhid_call(sc, parts, wq, wk, wv, x_mine, x_peer, dy_mine, dy_peer, bs_col, gain):
    rows, d = x_mine.shape
    nb = rows // HD
    pspec = pl.BlockSpec((HD, ROWS), lambda i, s: (((i // nb) * 2 + s[1]) * nb + i % nb, 0))
    slots = pltpu.VMEM((2, HD, d), BF)
    scratch = [pltpu.VMEM((HD, CHIP), BF), pltpu.VMEM((HD, ROWS), BF), pltpu.VMEM((HD, ROWS), BF)]
    scratch += [slots] * 5 + [pltpu.VMEM((8, d), F32), DMA((2, 2)), DMA((2, 2))]
    return launch(
        dhid_kernel, (2 * nb,),
        [pspec] * POOL + [whole(w.shape) for w in (wq, wk, wv)] + [whole((1, d)), whole(bs_col.shape)] + [ANY] * POOL,
        [ANY, ANY, once((1, d))], [((2 * rows, d),), ((rows, d),), ((1, d), F32)],
        (sc, *parts, wq, wk, wv, gain, bs_col, x_mine, x_peer, dy_mine, dy_peer),
        2 * 2 * rows * d * SEQ, rows * 2 * d * 8 + d * SEQ * 2, scratch=scratch,
    )


def gwp_kernel(
    sc, n0, n1, n2, n3, dm_o, dm_s, wp, pooled, gain, gq_x, gq_s, go_x, go_s, go_d, own_ref, sib_ref, *rest,
):
    half_ref, full_ref, dp_ref, gp_ref, fq, fo, acc, buf, sem, gsem = rest[2:]
    i = pid()
    used = sc[3 + i] > 0
    place = 3 + NQ + POOL
    jobs = zip((gq_x, gq_s, go_x, go_s, go_d), (fq, fq, fo, fo, fo))
    cps = placed([(src, dst, sc[place + n] + i * src.shape[0], slice(NONE)) for n, (src, dst) in enumerate(jobs)], sem)

    def rows_of_image(im, act):
        for t in range(2):
            b = jnp.minimum(sc[3 + NQ + 2 * im] + t, SEQ // HD - 1)
            r = b // POOL
            row = ((r // 2) * POOL + b % POOL) * HD
            for mine, src in (((r % 2) == sc[1], own_ref), ((r % 2) != sc[1], sib_ref)):

                @pl.when(mine)
                def _():
                    cp = pltpu.make_async_copy(src.at[at(row, HD), :], buf.at[im, pl.ds(HD * t, HD), :], gsem.at[im, t])
                    getattr(cp, act)()

    @pl.when(i == 0)
    def _():
        acc[ALL] = jnp.zeros_like(acc)
        for act in ("start", "wait"):
            for im in range(2):
                rows_of_image(im, act)
        row = iota((HD, HD2), 0)
        col = iota((HD, HD2), 1)
        g1 = ONE + gain[ALL]
        total = jnp.zeros_like(gain)
        for im in range(2):
            took = dot(onehot(col == row + sc[3 + NQ + 2 * im + 1]), buf[im]).astype(BF)
            cut = slice(HD * im, HD * im + HD)
            dn = dot_nt(took, wp[ALL]).astype(BF).astype(F32)
            pv = pooled[cut, :].astype(F32)
            rs = inv_rms(pv)
            n = pv * rs
            dnn = dn * n
            total = total + sum0(dnn)
            dp = ((dn * g1 - n * mean1(dnn * g1)) * rs).astype(BF).astype(F32)
            dp_ref[cut, :] = (dp * (ONE / SIDE)).astype(BF)
        gp_ref[ALL] = total

    @pl.when(used)
    def _():
        r = i // 2
        nrow = choose(r ^ sc[2], (n0, n1, n2, n3))
        acc[ALL] += dot_tn(nrow, jnp.where((r % 2) == sc[1], dm_o[ALL], dm_s[ALL]))

    @pl.when(i == pl.num_programs(0) - 1)
    def _():
        half_ref[ALL] = acc[ALL].astype(BF)
        full_ref[ALL] = acc[ALL].astype(BF)

    for cp in cps:
        cp.wait()


def gwp_call(sc, nrows, dm_own, dm_sib, wp, pooled, gain, pieces, fulls):
    dv, d = wp.shape
    cols = d // 2

    def nspec(n):
        return pl.BlockSpec((HD2, dv), lambda i, p: (jnp.where((i // 2) ^ p[2] == n, i % 2, 0), 0))

    dspec = pl.BlockSpec((HD2, cols), lambda i, p: ((i // POOL) * 2 + i % 2, p[1]))
    piece = lambda a: rowspec(a.shape[0] // NQ, a.shape[1])
    args = (sc, *nrows, dm_own, dm_sib, wp, pooled, gain, *pieces, dm_own, dm_sib, *fulls)
    n_in = len(args)
    ins = [nspec(n) for n in range(POOL)] + [dspec] * 2 + [whole(wp.shape), whole(pooled.shape), whole((1, dv))]
    ins += [piece(a) for a in pieces] + [ANY] * (2 + len(fulls))
    return launch(
        gwp_kernel, (NQ,), ins,
        [once((dv, cols)), pl.BlockSpec((dv, cols), lambda i, p: (0, p[1])), once(pooled.shape), once((1, dv))] + [ANY] * len(fulls),
        [((dv, cols),), ((dv, d),), (pooled.shape,), ((1, dv), F32)] + [(f.shape,) for f in fulls], args,
        SEQ * dv * d, SEQ * d * 2, alias=[(n_in - len(fulls) + n, POOL + n) for n in range(len(fulls))],
        scratch=[pltpu.VMEM((dv, cols), F32), pltpu.VMEM((2, HD2, d), BF), DMA((5,)), DMA((2, 2))],
    )


def dvis_kernel(sc, dp_ref, gp_s, gk_s, gv_s, gq_d, *rest):
    out_ref, fp, fk, fv, fq, sem = rest[-6:]
    i = pid()
    cols = pl.ds(pl.multiple_of(sc[0], LANES), gp_s.shape[1])
    cps = placed([(gp_s, fp, i * gp_s.shape[0], cols)], sem.at[pl.ds(0, 1)])
    jobs = ((gk_s, fk, sc[1]), (gv_s, fv, sc[1]), (gq_d, fq, sc[2]))
    cps += placed([(src, dst, row + i * src.shape[0], slice(NONE)) for src, dst, row in jobs], sem.at[pl.ds(1, 3)])
    row = iota((ROWS, GRID), 0)
    tok = iota((ROWS, GRID), 1)
    hit = (tok // SIDE == row // HD) & (tok % SIDE == (row % GRID) // POOL)
    out_ref[0] = dot(onehot(hit), dp_ref[ALL]).astype(BF)
    for cp in cps:
        cp.wait()


def dvis_call(sc, dp, pieces, fulls):
    n, dv = dp.shape
    spec = pl.BlockSpec((1, ROWS, dv), lambda i, s: (i // POOL, i % POOL, 0))
    ins = [rowspec(GRID, dv)] + [rowspec(a.shape[0] // NQ, a.shape[1]) for a in pieces] + [ANY] * POOL
    return launch(
        dvis_kernel, (NQ,), ins, [spec] + [ANY] * POOL,
        [((n // BLK, GRID * GRID, dv),)] + [(f.shape,) for f in fulls], (sc, dp, *pieces, *fulls),
        2 * n * SIDE * HD * dv, n * SIDE * dv * 2, alias=[(6 + n, 1 + n) for n in range(POOL)], scratch=[DMA((POOL,))],
    )


def solution(mesh):
    seq_spec = P(('dp', 'cp'))
    part_spec = P('dp')
    rep_spec = P()

    def body(vis, text, img_pos, grad_y, pn_gain, w_proj, pre_gain, w_query, w_key, w_value, q_gain, k_gain, w_out, post_gain):
        rank = lax.axis_index('cp')
        x = rank // 2
        c = rank % 2
        row_f32 = lambda g: g.astype(F32)[jnp.newaxis, :]
        ints = lambda *v: jnp.stack([jnp.asarray(e, jnp.int32) for e in v])

        def swap(a, perm):
            return lax.ppermute(a, 'cp', perm)

        pos = img_pos.astype(jnp.int32)
        here = pos[jnp.newaxis]
        ids = jnp.arange(pos.shape[0], dtype=jnp.int32)[jnp.newaxis]
        start = (jnp.arange(SEQ // HD, dtype=jnp.int32) * HD)[:, jnp.newaxis]

        def pick(hit):
            idx = jnp.sum(jnp.where(hit, ids, 0), axis=1)
            shift = jnp.where(jnp.any(hit, axis=1), start[:, 0] - jnp.sum(jnp.where(hit, here, 0), axis=1), FAR)
            return idx, shift

        ia, da = pick((here <= start) & (here + BLK > start))
        ib, db = pick((here > start) & (here < start + HD))
        tab = jnp.stack([ia, da, ib, db], axis=1).reshape(-1)
        used = jnp.minimum(da, db).reshape(NQ, -1).min(axis=1) < FAR
        rows = jnp.arange(SEQ, dtype=jnp.int32)
        inside = (rows[:, jnp.newaxis] >= here) & (rows[:, jnp.newaxis] < here + BLK)
        blk_start = jnp.where(jnp.any(inside, axis=1), jnp.sum(jnp.where(inside, here, 0), axis=1), -FAR)
        bs_col = blk_start[:, jnp.newaxis]
        bs_row = blk_start.reshape(NQ, 1, QB)
        nblk = jnp.arange(NQ, dtype=jnp.int32)
        edge = ((nblk + 1) * QB)[:, jnp.newaxis]
        cross = jnp.any((here < edge) & (here + BLK > edge), axis=1).astype(jnp.int32)
        nkv = nblk + 1 + cross
        first_q = nblk - jnp.concatenate([jnp.zeros((1,), jnp.int32), cross[:-1]])

        head_x = swap(text[:HD], XPERM)
        pooled, normed = pool_call(vis, row_f32(pn_gain))
        normed_x = swap(normed, XPERM)
        rest_x = swap(text[HD:], XPERM)
        dy_x = swap(grad_y, XPERM)
        theirs = swap(jnp.stack([normed, normed_x]), SPERM)
        normed_all = jnp.zeros((POOL,) + normed.shape, BF)
        for piece, slot in ((normed, 0), (normed_x, 2), (theirs[0], 1), (theirs[1], 3)):
            normed_all = lax.dynamic_update_index_in_dim(normed_all, piece, rank ^ slot, 0)
        normed_all = normed_all.reshape(-1, normed.shape[1])

        pre = row_f32(pre_gain)
        qg, kg = row_f32(q_gain), row_f32(k_gain)
        x_mine, h_mine, n_mine = merge_call(tab, ints(rank), normed_all, w_proj, pre, text, text)
        h_sib = swap(h_mine, SPERM)
        inv_freq = ROPE_BASE ** (-jnp.arange(0, HD, 2).astype(F32) / HD)
        angle = (rows.astype(F32) / ROPE_SCALE)[:, jnp.newaxis] * inv_freq[jnp.newaxis, :]
        cos, sin = jnp.cos(angle), jnp.sin(angle)
        qkv_args = (w_query, w_key, w_value, qg, kg, cos, sin)
        bufs = qkv_call(ints(x, c), h_mine, h_sib, *qkv_args, ())
        x_peer, h_peer, n_peer = merge_call(tab, ints(rank ^ 2), normed_all, w_proj, pre, head_x, rest_x)
        h_diag = swap(h_peer, SPERM)
        n_sib = swap(n_mine, SPERM)
        n_diag = swap(n_peer, SPERM)
        q0, q1, qr0, qr1, k0, k1, kr0, kr1, v0, v1 = qkv_call(ints(1 - x, c), h_peer, h_diag, *qkv_args, bufs)

        o0, lse0 = fwd_call(nkv, q0, k0, v0, bs_col)
        o0s = swap(o0, SPERM)
        o1, lse1 = fwd_call(nkv, q1, k1, v1, bs_col)
        o1s = swap(o1, SPERM)

        post = row_f32(post_gain)
        y, dp_m, dam0, dam1, das0, das1, gpost_m = out_call(ints(x, c), (o0, o1), (o0s, o1s), w_out, grad_y, post, (x_mine,))
        das0, das1 = swap(das0, SPERM), swap(das1, SPERM)
        dp_sm = swap(dp_m, SPERM)
        dp_p, dap0, dap1, dbs0, dbs1, gpost_p = out_call(ints(1 - x, c), (o0, o1), (o0s, o1s), w_out, dy_x, post)
        dbs0, dbs1 = swap(dbs0, SPERM), swap(dbs1, SPERM)
        dp_sp = swap(dp_p, SPERM)

        bsc = jnp.concatenate([ints(rank), first_q])
        bwd_args = (cos, sin, qg, kg)
        part0, gq0, gk0 = bwd_call(bsc, q0, (dam0, dap0, das0, dbs0), o0, k0, v0, lse0, bs_row, qr0, kr0, *bwd_args)
        part0s = swap(part0, SPERM)
        part1, gq1, gk1 = bwd_call(bsc, q1, (dam1, dap1, das1, dbs1), o1, k1, v1, lse1, bs_row, qr1, kr1, *bwd_args)
        part1s = swap(part1, SPERM)
        early = jnp.concatenate([gq0 + gq1, gk0 + gk1, gpost_m + gpost_p], axis=1)
        early = early + swap(early, SPERM)

        go, go_full = gwo_call(ints(x, c, rank, *[rank ^ n for n in SLOT]), o0, o1, (dp_m, dp_p, dp_sm, dp_sp))
        go_x = swap(go, XPERM)
        go_s = swap(go, SPERM)
        parts = (part0, part1, part0s, part1s)
        hids = (h_mine, h_sib, h_peer, h_diag)
        gq, gq_full = gw_call(ints(x, c, rank), hids, parts, 0)
        gq_x = swap(gq, XPERM)
        gq_s = swap(gq, SPERM)
        dm, grad_text, gpre = dhid_call(ints(x, c), parts, w_query, w_key, w_value, x_mine, x_peer, grad_y, dy_x, bs_col, pre)
        dm_s = swap(dm, SPERM)
        go_d = swap(go_x, SPERM)
        gpre = gpre + swap(gpre, SPERM)
        gk, gv, gk_full, gv_full = gw_call(ints(x, c, rank), hids, parts, 1)
        gq_d = swap(gq_x, SPERM)
        gk_s, gv_s = swap(gk, SPERM), swap(gv, SPERM)
        mine = lax.dynamic_slice_in_dim(pos, 2 * rank, 2)
        quarter = w_query.shape[0] // POOL
        spots = [(rank ^ n) * quarter for n in (2, 1)] + [(2 * c + 1 - x) * HD2, (2 - 2 * c + x) * HD2, (3 - 2 * c - x) * HD2]
        psc = jnp.concatenate([ints(x, c, rank), used.astype(jnp.int32), jnp.stack([mine // HD, mine % HD], axis=1).reshape(-1), ints(*spots)])
        gp, gp_full, dpool, gpn, gq_full, g_out = gwp_call(
            psc, (n_mine, n_sib, n_peer, n_diag), dm, dm_s, w_proj, pooled, row_f32(pn_gain), (gq_x, gq_s, go_x, go_s, go_d),
            (gq_full, go_full),
        )
        gp_s = swap(gp, SPERM)
        gpn = gpn + swap(gpn, XPERM)
        gpn = gpn + swap(gpn, SPERM)
        spots = ints((1 - c) * gp.shape[1], (1 - c) * 2 * quarter, (rank ^ 3) * quarter)
        grad_vis, g_proj, gk, gv, gq = dvis_call(spots, dpool, (gp_s, gk_s, gv_s, gq_d), (gp_full, gk_full, gv_full, gq_full))

        early = early[0].astype(BF)
        sq, sk, spost = early[:HD], early[HD:HD2], early[HD2:]
        return (y, grad_text, grad_vis, gpn[0].astype(BF), g_proj, gpre[0].astype(BF), gq, gk, gv, sq, sk, g_out, spost)

    in_specs = (seq_spec, seq_spec, part_spec, seq_spec) + (rep_spec,) * 10
    out_specs = (seq_spec, seq_spec, seq_spec) + (part_spec,) * 10
    return jax.shard_map(body, mesh=mesh, in_specs=in_specs, out_specs=out_specs, check_vma=not YES)
```

time: 2450 us -> 987 us (0.40)
  blocking collectives: 1260 us -> 0 us
  matrix products: 766 us -> 0 us
  Pallas kernels: 0 us -> 656 us
  waiting for transfers between devices: 87.9 us -> 257 us
  local copies, waits for them, and re-layouts: 164 us -> 25.4 us
  other arithmetic: 141 us -> 19.1 us
    psum x1 -> x0, blocking collectives: 1260 us -> none  [device_body(): lax.psum((g_pn, g_proj, g_pre, g_query, g_key, g_value, g_q_gain, g_k_gai...]
    dot_general x20 -> x0, matrix products: 699 us -> none  [the longest x1 177 us: attn_backward(): jnp.einsum('kgqs,skd->qkgd', d_scores, k_all, preferred_element_type=jnp....]
    pallas_call x0 -> x17, Pallas kernels: none -> 656 us  [launch(): pl.pallas_call(kernel, grid_spec=pltpu.PrefetchScalarGridSpec(num_scalar_...]
    ppermute x0 -> x33, waiting for transfers between devices: none -> 257 us  [swap(): return lax.ppermute(a, 'cp', perm)]
    sub x1 -> x0, matrix products: 67.6 us -> none  [attn_forward(): probs_hi = jax.nn.softmax(jnp.where(visible, scores, NEG_BIG), axis=-1)]
    all_gather x3 -> x0, waiting for transfers between devices: 65.6 us -> none  [the longest x1 65.6 us: device_body(): soft_all = lax.all_gather(soft_loc, 'cp', tiled=True)]
    convert_element_type x5 -> x0, local copies, waits for them, and re-layouts: 59.9 us -> none  [the longest x1 34.8 us: pool_patches(): pooled = jnp.sum(patch_grid, axis=(2, 4), dtype=jnp.float32) / (POOL * POOL)]
    reduce_sum x8 -> x2, other arithmetic: 48.7 us -> 0.21 us  [the longest x1 0.12 us: body(): jnp.sum(jnp.where(inside, here, 0), axis=1)]
  transfers between devices with their start and end apart: 6 -> 33, of which waited for: 2 -> 12; matrix products, arithmetic and copies ran while one was open for 28% -> 4% of each run, Pallas kernels for 0% -> 57%
where the time goes in v1:
time: 987 us; the launch traced here: 979 us
  Pallas kernels  656 us (66%)
  waiting for transfers between devices  257 us (26%)
  local copies, waits for them, and re-layouts  25.4 us (3%)
  starting transfers between devices  20 us (2%)
  other arithmetic  19.1 us (2%)
    pallas_call x17, Pallas kernels, launch(): pl.pallas_call(kernel, grid_spec=pltpu.PrefetchScalarGridSpec(num_scalar_...  656 us
    ppermute x33, waiting for transfers between devices, swap(): return lax.ppermute(a, 'cp', perm)  257 us
    ppermute x33, starting transfers between devices, swap(): return lax.ppermute(a, 'cp', perm)  20 us
  transfers between devices with their start and end apart: 33, of which 12 were waited for; matrix products, arithmetic and copies ran while one was open for 4% of the time, Pallas kernels for 57%

profile of v1, /device:TPU:0, one launch (start us, length us, event | category | flops | bytes accessed | tf_op | source)
XLA Modules:
  0.0 979.1 jit_solution(17093547187669362153)
XLA Ops:
  0.6 1.3 reshape.146.gain_ref.gain
  1.9 11.4 %shard_map.237 = (bf16[512,1152]{1,0:T(8,128)(2,1)}, bf16[512,1152]{1,0:T(8,128)(2,1)}) custom-call(bf16[2,4096,1152]{2,1,0:T(8,128)(2,1)} %vis_ref.1, f32[1,1152]{1,0:T(1,128)} %reshape.146.gain_ref.gain), custom_call_target="tpu_custom_call" | custom-call | flops 1207959552 | bytes 18874368 | tf_op jit(solution)/shard_map/pallas_call | solution.py:105
  13.4 3.3 collective-permute-start
  16.7 26.2 %collective-permute-done = bf16[512,1152]{1,0:T(8,128)(2,1)S(1)} collective-permute-done((bf16[512,1152]{1,0:T(8,128)(2,1)}, bf16[512,1152]{1,0:T(8,128)(2,1)S(1)}, u32[]{:S(2)}, u32[]{:S(2)}) %collective-permute-start) | collective-permute-done | bytes 1179680 | tf_op jit(solution)/shard_map/ppermute | solution.py:784
  42.9 2.9 pad_maximum_fusion
  45.8 4.3 slice.36
  50.1 1.7 collective-permute-start.3
  52.1 2.5 broadcast_in_dim.98
  54.6 1.1 constant_dynamic-update-slice_fusion.1
  55.8 0.6 reshape.143.tab
  56.4 0.6 reshape.147.gain
  57.0 1.1 constant_dynamic-update-slice_fusion
  58.1 2.4 slice_dynamic-update-slice_fusion.1
  60.5 2.4 slice_dynamic-update-slice_fusion
  62.9 14.3 %shard_map.239 = (bf16[1024,2560]{1,0:T(8,128)(2,1)}, bf16[1024,2560]{1,0:T(8,128)(2,1)}, bf16[1024,1152]{1,0:T(8,128)(2,1)}) custom-call(s32[64]{0:T(128)} %reshape.143.tab, s32[1]{0:T(128)} %bitcast.15.sc, bf16[2048,1152]{1,0:T(8,128)(2,1)} %bitcast.12.normed, bf16[1152,2560]{1,0:T(8,128)(2,1)} %wp.5, f32[1,2560]{1,0:T(1,128)} %reshape.147.gain, ...), custom_call_target="tpu_custom_call" | custom-call | flops 7247757312 | bytes 21626880 | tf_op jit(solution)/shard_map/pallas_call | solution.py:105
  77.2 4.4 collective-permute-start.5
  81.6 1.4 slice.35
  83.3 82.4 %collective-permute-done.2.ta = bf16[256,2560]{1,0:T(8,128)(2,1)S(1)} collective-permute-done((bf16[256,2560]{1,0:T(8,128)(2,1)S(1)}, bf16[256,2560]{1,0:T(8,128)(2,1)S(1)}, u32[]{:S(2)}, u32[]{:S(2)}) %collective-permute-start.2) | collective-permute-done | bytes 1310752 | tf_op jit(solution)/shard_map/ppermute | solution.py:784
  165.7 1.1 copy-done.22
  166.8 18.6 %shard_map.238 = (bf16[1024,2560]{1,0:T(8,128)(2,1)}, bf16[1024,2560]{1,0:T(8,128)(2,1)}, bf16[1024,1152]{1,0:T(8,128)(2,1)}) custom-call(s32[64]{0:T(128)} %reshape.143.tab, s32[1]{0:T(128)} %bitcast.9.sc, bf16[2048,1152]{1,0:T(8,128)(2,1)} %bitcast.12.normed, bf16[1152,2560]{1,0:T(8,128)(2,1)} %wp.5, f32[1,2560]{1,0:T(1,128)} %reshape.147.gain, ...), custom_call_target="tpu_custom_call" | custom-call | flops 7247757312 | bytes 21626880 | tf_op jit(solution)/shard_map/pallas_call | solution.py:105
  185.4 1.4 collective-permute-start.8
  186.8 0.6 broadcast_in_dim.116
  187.3 0.6 broadcast_in_dim.117
  188.2 2.0 copy.51.bs_ref.bs
  190.2 0.6 pad_add_fusion.3.sc
  190.8 0.6 pad_add_fusion.2.sc
  192.1 9.3 multiply_sine_fusion
  201.4 33.1 %shard_map.240 = (bf16[4096,512]{1,0:T(8,128)(2,1)}, bf16[4096,512]{1,0:T(8,128)(2,1)}, bf16[4096,512]{1,0:T(8,128)(2,1)}, bf16[4096,512]{1,0:T(8,128)(2,1)}, bf...) custom-call(s32[2]{0:T(128)} %pad_add_fusion.2.sc, ...), custom_call_target="tpu_custom_call" | custom-call | flops 21474836480 | bytes 33554432 | tf_op jit(solution)/shard_map/pallas_call | solution.py:105
  234.5 32.8 %shard_map.241 = (bf16[4096,512]{1,0:T(8,128)(2,1)}, bf16[4096,512]{1,0:T(8,128)(2,1)}, bf16[4096,512]{1,0:T(8,128)(2,1)}, bf16[4096,512]{1,0:T(8,128)(2,1)}, bf...) custom-call(s32[2]{0:T(128)} %pad_add_fusion.3.sc, ...), custom_call_target="tpu_custom_call", output_to_operand_aliasing={{0}: (10, {}), {1}: (11, {}), {2}: (12, {}), {3}: (13, {}),... | custom-call | flops 21474836480 | bytes 33554432 | tf_op jit(solution)/shard_map/pallas_call | solution.py:105
  267.3 46.6 %shard_map.242 = (bf16[4096,512]{1,0:T(8,128)(2,1)}, f32[8,2,512]{2,1,0:T(2,128)}) custom-call(s32[8]{0:T(128)} %fusion.5.nkv, bf16[4096,512]{1,0:T(8,128)(2,1)} %get-tuple-element.99.q_ref, bf16[4096,256]{1,0:T(8,128)(2,1)} %get-tuple-element.100.k_ref, bf16[4096,256]{1,0:T(8,128)(2,1)} %get-tuple-element.101.v_ref, s32[4096,1]{1,0:T(8,128)} %copy.51.bs_ref.bs), custom_call_target="tpu_custom_call" | custom-call | flops 21474836480 | bytes 12582912 | tf_op jit(solution)/shard_map/pallas_call | solution.py:105
  313.9 46.5 %shard_map.243 = (bf16[4096,512]{1,0:T(8,128)(2,1)}, f32[8,2,512]{2,1,0:T(2,128)}) custom-call(s32[8]{0:T(128)} %fusion.5.nkv, bf16[4096,512]{1,0:T(8,128)(2,1)} %get-tuple-element.103.q_ref, bf16[4096,256]{1,0:T(8,128)(2,1)} %get-tuple-element.104.k_ref, bf16[4096,256]{1,0:T(8,128)(2,1)} %get-tuple-element.105.v_ref, s32[4096,1]{1,0:T(8,128)} %copy.51.bs_ref.bs), custom_call_target="tpu_custom_call" | custom-call | flops 21474836480 | bytes 12582912 | tf_op jit(solution)/shard_map/pallas_call | solution.py:105
  361.0 0.6 reshape.150.gain
  361.6 6.5 collective-permute-done.7.os1
  368.1 34.2 %shard_map.245 = (bf16[1024,2560]{1,0:T(8,128)(2,1)}, bf16[1024,512]{1,0:T(8,128)(2,1)}, bf16[1024,512]{1,0:T(8,128)(2,1)}, bf16[1024,512]{1,0:T(8,128)(2,1)}, b...) custom-call(s32[2]{0:T(128)} %pad_add_fusion.3.sc, bf16[4096,512]{1,0:T(8,128)(2,1)} %get-tuple-element.102.oo0.o_ref.o0, ...), custom_call_target="tpu_custom_call" | custom-call | flops 21474836480 | bytes 36700160 | tf_op jit(solution)/shard_map/pallas_call | solution.py:105
  402.6 36.7 %shard_map.244 = (bf16[1024,2560]{1,0:T(8,128)(2,1)}, bf16[1024,2560]{1,0:T(8,128)(2,1)}, bf16[1024,512]{1,0:T(8,128)(2,1)}, bf16[1024,512]{1,0:T(8,128)(2,1)}, ...) custom-call(s32[2]{0:T(128)} %pad_add_fusion.2.sc, ...), custom_call_target="tpu_custom_call" | custom-call | flops 21474836480 | bytes 36700160 | tf_op jit(solution)/shard_map/pallas_call | solution.py:105
  439.6 0.6 pad_add_fusion.4.sc
  440.7 1.7 collective-permute-done.11.do_c
  442.3 86.4 %shard_map.247 = (bf16[4096,1024]{1,0:T(8,128)(2,1)}, f32[1,256]{1,0:T(1,128)}, f32[1,256]{1,0:T(1,128)}) custom-call(s32[9]{0:T(128)} %pad_add_fusion.4.sc, bf16[4096,512]{1,0:T(8,128)(2,1)} %get-tuple-element.103.q_ref, bf16[1024,512]{1,0:T(8,128)(2,1)} %get-tuple-element.117.do_a, bf16[1024,512]{1,0:T(8,128)(2,1)} %get-tuple-element.118.do_b, ...), custom_call_target="tpu_custom_call" | custom-call | flops 51539607552 | bytes 33554432 | tf_op jit(solution)/shard_map/pallas_call | solution.py:105
  529.0 1.0 copy-done.23
  529.9 86.6 %shard_map.246 = (bf16[4096,1024]{1,0:T(8,128)(2,1)}, f32[1,256]{1,0:T(1,128)}, f32[1,256]{1,0:T(1,128)}) custom-call(s32[9]{0:T(128)} %pad_add_fusion.4.sc, bf16[4096,512]{1,0:T(8,128)(2,1)} %get-tuple-element.99.q_ref, bf16[1024,512]{1,0:T(8,128)(2,1)} %get-tuple-element.109.do_a, bf16[1024,512]{1,0:T(8,128)(2,1)} %get-tuple-element.110.do_b, ...), custom_call_target="tpu_custom_call" | custom-call | flops 51539607552 | bytes 33554432 | tf_op jit(solution)/shard_map/pallas_call | solution.py:105
  617.4 12.6 %collective-permute-done.13.s0.refs_6_ = bf16[4096,1024]{1,0:T(8,128)(2,1)} collective-permute-done((bf16[4096,1024]{1,0:T(8,128)(2,1)}, bf16[4096,1024]{1,0:T(8,128)(2,1)}, u32[]{:S(2)}, u32[]{:S(2)}) %collective-permute-start.13) | collective-permute-done | bytes 8388640 | tf_op jit(solution)/shard_map/ppermute | solution.py:784
  630.0 74.7 %shard_map.248 = (bf16[2048,2560]{1,0:T(8,128)(2,1)}, bf16[1024,2560]{1,0:T(8,128)(2,1)}, f32[1,2560]{1,0:T(1,128)}) custom-call(s32[2]{0:T(128)} %pad_add_fusion.2.sc, bf16[4096,1024]{1,0:T(8,128)(2,1)} %get-tuple-element.116.p0.refs_4_, bf16[4096,1024]{1,0:T(8,128)(2,1)} %get-tuple-element.124.p1.refs_5_, ...), custom_call_target="tpu_custom_call" | custom-call | flops 42949672960 | bytes 62914560 | tf_op jit(solution)/shard_map/pallas_call | solution.py:105
  705.2 0.6 stack.134.sc
  705.8 22.7 %shard_map.250 = (bf16[512,2560]{1,0:T(8,128)(2,1)}, bf16[2048,2560]{1,0:T(8,128)(2,1)}) custom-call(s32[7]{0:T(128)} %stack.134.sc, bf16[4096,512]{1,0:T(8,128)(2,1)} %get-tuple-element.102.oo0.o_ref.o0, bf16[4096,512]{1,0:T(8,128)(2,1)} %get-tuple-element.106.oo1.o_ref.o1, bf16[1024,2560]{1,0:T(8,128)(2,1)} %get-tuple-element.132.dp0, ...), custom_call_target="tpu_custom_call" | custom-call | flops 10737418240 | bytes 29360128 | tf_op jit(solution)/shard_map/pallas_call | solution.py:105
  728.5 1.1 collective-permute-start.22
  730.1 0.6 pad_add_fusion.6.sc
  730.8 56.9 %collective-permute-done.22.go_x = bf16[512,2560]{1,0:T(8,128)(2,1)} collective-permute-done((bf16[512,2560]{1,0:T(8,128)(2,1)}, bf16[512,2560]{1,0:T(8,128)(2,1)}, u32[]{:S(2)}, u32[]{:S(2)}) %collective-permute-start.22) | collective-permute-done | bytes 2621472 | tf_op jit(solution)/shard_map/ppermute | solution.py:784
  787.7 19.7 %shard_map.249 = (bf16[640,2048]{1,0:T(8,128)(2,1)}, bf16[2560,2048]{1,0:T(8,128)(2,1)}) custom-call(s32[3]{0:T(128)} %pad_add_fusion.6.sc, bf16[1024,2560]{1,0:T(8,128)(2,1)} %get-tuple-element.88.ha.refs_0_, bf16[1024,2560]{1,0:T(8,128)(2,1)} %collective-permute-done.5.hb.refs_1_, bf16[1024,2560]{1,0:T(8,128)(2,1)} %get-tuple-element.87.ha.refs_2_, ...), custom_call_target="tpu_custom_call" | custom-call | flops 10737418240 | bytes 22020096 | tf_op jit(solution)/shard_map/pallas_call | solution.py:105
  807.9 1.2 collective-permute-start.18
  809.8 0.6 concatenate.14.sc
  810.5 2.3 collective-permute-done.19.gq_s
  812.8 54.3 %collective-permute-done.18.gq_x = bf16[640,2048]{1,0:T(8,128)(2,1)} collective-permute-done((bf16[640,2048]{1,0:T(8,128)(2,1)}, bf16[640,2048]{1,0:T(8,128)(2,1)}, u32[]{:S(2)}, u32[]{:S(2)}) %collective-permute-start.18) | collective-permute-done | bytes 2621472 | tf_op jit(solution)/shard_map/ppermute | solution.py:784
  867.0 37.9 %shard_map.251 = (bf16[1152,1280]{1,0:T(8,128)(2,1)}, bf16[1152,2560]{1,0:T(8,128)(2,1)}, bf16[512,1152]{1,0:T(8,128)(2,1)}, f32[1,1152]{1,0:T(1,128)}, bf16[256...) custom-call(s32[20]{0:T(128)} %concatenate.14.sc, ...), custom_call_target="tpu_custom_call", output_to_operand_aliasing={{4}: (17, {}), {5}: (18, {})} | custom-call | flops 12079595520 | bytes 20971520 | tf_op jit(solution)/shard_map/pallas_call | solution.py:105
  905.0 36.8 %shard_map.252 = (bf16[1280,1024]{1,0:T(8,128)(2,1)}, bf16[1280,1024]{1,0:T(8,128)(2,1)}, bf16[2560,1024]{1,0:T(8,128)(2,1)}, bf16[2560,1024]{1,0:T(8,128)(2,1)}) custom-call(s32[3]{0:T(128)} %pad_add_fusion.6.sc, bf16[1024,2560]{1,0:T(8,128)(2,1)} %get-tuple-element.88.ha.refs_0_, bf16[1024,2560]{1,0:T(8,128)(2,1)} %collective-permute-done.5.hb.refs_1_, ...), custom_call_target="tpu_custom_call" | custom-call | flops 21474836480 | bytes 44040192 | tf_op jit(solution)/shard_map/pallas_call | solution.py:105
  941.8 0.5 collective-permute-start.26
  943.0 0.6 pad_add_fusion.5.sc
  943.6 11.1 %collective-permute-done.32 = f32[1,3072]{1,0:T(1,128)S(1)} collective-permute-done((f32[1,3072]{1,0:T(1,128)S(1)}, f32[1,3072]{1,0:T(1,128)S(1)}, u32[]{:S(2)}, u32[]{:S(2)}) %collective-permute-start.32) | collective-permute-done | bytes 12320 | tf_op jit(solution)/shard_map/ppermute | solution.py:784
  954.8 1.2 collective-permute-start.29
  955.9 0.6 slice_reduce_fusion
  956.6 1.8 collective-permute-done.29
  959.0 0.6 collective-permute-done.31
  959.8 0.6 convert_reduce_fusion
  960.8 0.6 convert_reduce_fusion.1
  961.4 17.4 %shard_map.253 = (bf16[2,4096,1152]{2,1,0:T(8,128)(2,1)}, bf16[1152,2560]{1,0:T(8,128)(2,1)}, bf16[2560,1024]{1,0:T(8,128)(2,1)}, bf16[2560,1024]{1,0:T(8,128)(2,1)}, bf16[2560,2048]{1,0:T(8,128)(2,1)}) custom-call(s32[3]{0:T(128)} %pad_add_fusion.5.sc, ...), custom_call_target="tpu_custom_call", output_to_operand_aliasing={{1}: (6, {}), {2}: (7, {}), {3}: (8, {}), {4}: (9, {})} | custom-call | flops 4831838208 | bytes 18874368 | tf_op jit(solution)/shard_map/pallas_call | solution.py:105
  (132 shorter events, 8.4 us)
Async XLA Ops:
  13.4 29.5 %collective-permute-start = (bf16[512,1152]{1,0:T(8,128)(2,1)}, bf16[512,1152]{1,0:T(8,128)(2,1)S(1)}, u32[]{:S(2)}, u32[]{:S(2)}) collective-permute-start(bf16[512,1152]{1,0:T(8,128)(2,1)} %get-tuple-element.86), channel_id=1, source_target_pairs={{0,2},{2,0},{1,3},{3,1},{4,6},{6,4},{5,7},{7,5}} | collective-permute-start | bytes 3538952 | tf_op jit(solution)/shard_map/ppermute | solution.py:784
  45.8 6.1 copy-start.2
  45.8 12.4 %collective-permute-start.1 = (bf16[2,512,1152]{2,1,0:T(8,128)(2,1)}, bf16[2,512,1152]{2,1,0:T(8,128)(2,1)}, u32[]{:S(2)}, u32[]{:S(2)}) collective-permute-start(bf16[2,512,1152]{2,1,0:T(8,128)(2,1)} %pad_maximum_fusion), channel_id=1, source_target_pairs={{0,1},{1,0},{2,3},{3,2},{4,5},{5,4},{6,7},{7,6}} | collective-permute-start | bytes 7077896 | tf_op jit(solution)/shard_map/ppermute | solution.py:784
  50.1 4.5 copy-start
  50.1 6.3 copy-start.7
  50.1 116.7 %collective-permute-start.3 = (bf16[768,2560]{1,0:T(8,128)(2,1)}, bf16[768,2560]{1,0:T(8,128)(2,1)}, u32[]{:S(2)}, u32[]{:S(2)}) collective-permute-start(bf16[768,2560]{1,0:T(8,128)(2,1)} %slice.36), channel_id=1, source_target_pairs={{0,2},{2,0},{1,3},{3,1},{4,6},{6,4},{5,7},{7,5}} | collective-permute-start | bytes 11796488 | tf_op jit(solution)/shard_map/ppermute | solution.py:784
  51.9 6.2 copy-start.18
  51.9 6.2 copy-start.20
  52.0 6.1 copy-start.10
  52.0 6.1 copy-start.12
  77.2 124.2 %collective-permute-start.5 = (bf16[1024,2560]{1,0:T(8,128)(2,1)}, bf16[1024,2560]{1,0:T(8,128)(2,1)}, u32[]{:S(2)}, u32[]{:S(2)}) collective-permute-start(bf16[1024,2560]{1,0:T(8,128)(2,1)} %get-tuple-element.88.ha.refs_0_), channel_id=1, source_target_pairs={{0,1},{1,0},{2,3},{3,2},{4,5},{5,4},{6,7},{7,6}} | collective-permute-start | bytes 15728648 | tf_op jit(solution)/shard_map/ppermute | solution.py:784
  83.0 82.7 %collective-permute-start.2 = (bf16[256,2560]{1,0:T(8,128)(2,1)S(1)}, bf16[256,2560]{1,0:T(8,128)(2,1)S(1)}, u32[]{:S(2)}, u32[]{:S(2)}) collective-permute-start(bf16[256,2560]{1,0:T(8,128)(2,1)S(1)} %slice.35), channel_id=1, source_target_pairs={{0,2},{2,0},{1,3},{3,1},{4,6},{6,4},{5,7},{7,5}} | collective-permute-start | bytes 3932168 | tf_op jit(solution)/shard_map/ppermute | solution.py:784
  165.7 1.1 copy-start.22
  166.8 20.0 %copy-start.24 = (bf16[256]{0:T(256)(128)(2,1)S(1)}, bf16[256]{0:T(256)(128)(2,1)}, u32[]{:S(2)}) copy-start(bf16[256]{0:T(256)(128)(2,1)} %param.24) | copy-start | bytes 1540
  166.8 20.6 %copy-start.25 = (bf16[256]{0:T(256)(128)(2,1)S(1)}, bf16[256]{0:T(256)(128)(2,1)}, u32[]{:S(2)}) copy-start(bf16[256]{0:T(256)(128)(2,1)} %param.25) | copy-start | bytes 1540
  185.4 49.1 %collective-permute-start.4 = (bf16[1024,2560]{1,0:T(8,128)(2,1)}, bf16[1024,2560]{1,0:T(8,128)(2,1)}, u32[]{:S(2)}, u32[]{:S(2)}) collective-permute-start(bf16[1024,2560]{1,0:T(8,128)(2,1)} %get-tuple-element.87.ha.refs_2_), channel_id=1, source_target_pairs={{0,1},{1,0},{2,3},{3,2},{4,5},{5,4},{6,7},{7,6}} | collective-permute-start | bytes 15728648 | tf_op jit(solution)/shard_map/ppermute | solution.py:784
  185.4 176.2 %collective-permute-start.8 = (bf16[1024,2560]{1,0:T(8,128)(2,1)}, bf16[1024,2560]{1,0:T(8,128)(2,1)}, u32[]{:S(2)}, u32[]{:S(2)}) collective-permute-start(bf16[1024,2560]{1,0:T(8,128)(2,1)} %dya.1), channel_id=1, source_target_pairs={{0,2},{2,0},{1,3},{3,1},{4,6},{6,4},{5,7},{7,5}} | collective-permute-start | bytes 15728648 | tf_op jit(solution)/shard_map/ppermute | solution.py:784
  188.2 46.3 %copy-start.1 = (s32[4096]{0:T(1024)}, s32[4096]{0:T(1024)S(1)}, u32[]{:S(2)}) copy-start(s32[4096]{0:T(1024)S(1)} %broadcast_select_fusion) | copy-start | bytes 49156
  313.9 47.6 %collective-permute-start.6 = (bf16[4096,512]{1,0:T(8,128)(2,1)}, bf16[4096,512]{1,0:T(8,128)(2,1)}, u32[]{:S(2)}, u32[]{:S(2)}) collective-permute-start(bf16[4096,512]{1,0:T(8,128)(2,1)} %get-tuple-element.102.oo0.o_ref.o0), channel_id=1, source_target_pairs={{0,1},{1,0},{2,3},{3,2},{4,5},{5,4},{6,7},{7,6}} | collective-permute-start | bytes 12582920 | tf_op jit(solution)/shard_map/ppermute | solution.py:784
  313.9 47.0 %copy-start.8 = (bf16[2560]{0:T(1024)(128)(2,1)S(1)}, bf16[2560]{0:T(1024)(128)(2,1)}, u32[]{:S(2)}) copy-start(bf16[2560]{0:T(1024)(128)(2,1)} %param.27) | copy-start | bytes 15364
  360.5 7.6 collective-permute-start.7
  402.2 38.4 %collective-permute-start.12 = (bf16[1024,512]{1,0:T(8,128)(2,1)}, bf16[1024,512]{1,0:T(8,128)(2,1)}, u32[]{:S(2)}, u32[]{:S(2)}) collective-permute-start(bf16[1024,512]{1,0:T(8,128)(2,1)} %get-tuple-element.120), channel_id=1, source_target_pairs={{0,1},{1,0},{2,3},{3,2},{4,5},{5,4},{6,7},{7,6}} | collective-permute-start | bytes 3145736 | tf_op jit(solution)/shard_map/ppermute | solution.py:784
  439.3 3.0 collective-permute-start.11
  440.2 88.8 %collective-permute-start.10 = (bf16[1024,512]{1,0:T(8,128)(2,1)}, bf16[1024,512]{1,0:T(8,128)(2,1)S(1)}, u32[]{:S(2)}, u32[]{:S(2)}) collective-permute-start(bf16[1024,512]{1,0:T(8,128)(2,1)} %get-tuple-element.112), channel_id=1, source_target_pairs={{0,1},{1,0},{2,3},{3,2},{4,5},{5,4},{6,7},{7,6}} | collective-permute-start | bytes 3145736 | tf_op jit(solution)/shard_map/ppermute | solution.py:784
  440.5 88.4 %collective-permute-start.9 = (bf16[1024,512]{1,0:T(8,128)(2,1)}, bf16[1024,512]{1,0:T(8,128)(2,1)}, u32[]{:S(2)}, u32[]{:S(2)}) collective-permute-start(bf16[1024,512]{1,0:T(8,128)(2,1)} %get-tuple-element.111), channel_id=1, source_target_pairs={{0,1},{1,0},{2,3},{3,2},{4,5},{5,4},{6,7},{7,6}} | collective-permute-start | bytes 3145736 | tf_op jit(solution)/shard_map/ppermute | solution.py:784
  528.8 88.6 %collective-permute-start.14 = (bf16[4096,1024]{1,0:T(8,128)(2,1)}, bf16[4096,1024]{1,0:T(8,128)(2,1)}, u32[]{:S(2)}, u32[]{:S(2)}) collective-permute-start(bf16[4096,1024]{1,0:T(8,128)(2,1)} %get-tuple-element.124.p1.refs_5_), channel_id=1, source_target_pairs={{0,1},{1,0},{2,3},{3,2},{4,5},{5,4},{6,7},{7,6}} | collective-permute-start | bytes 25165832 | tf_op jit(solution)/shard_map/ppermute | solution.py:784
  529.0 1.0 copy-start.23
  616.5 13.5 %collective-permute-start.13 = (bf16[4096,1024]{1,0:T(8,128)(2,1)}, bf16[4096,1024]{1,0:T(8,128)(2,1)}, u32[]{:S(2)}, u32[]{:S(2)}) collective-permute-start(bf16[4096,1024]{1,0:T(8,128)(2,1)} %get-tuple-element.116.p0.refs_4_), channel_id=1, source_target_pairs={{0,1},{1,0},{2,3},{3,2},{4,5},{5,4},{6,7},{7,6}} | collective-permute-start | bytes 25165832 | tf_op jit(solution)/shard_map/ppermute | solution.py:784
  616.9 88.9 %collective-permute-start.21 = (bf16[1024,2560]{1,0:T(8,128)(2,1)}, bf16[1024,2560]{1,0:T(8,128)(2,1)}, u32[]{:S(2)}, u32[]{:S(2)}) collective-permute-start(bf16[1024,2560]{1,0:T(8,128)(2,1)} %get-tuple-element.133.dp1), channel_id=1, source_target_pairs={{0,1},{1,0},{2,3},{3,2},{4,5},{5,4},{6,7},{7,6}} | collective-permute-start | bytes 15728648 | tf_op jit(solution)/shard_map/ppermute | solution.py:784
  617.0 88.8 %collective-permute-start.20 = (bf16[1024,2560]{1,0:T(8,128)(2,1)}, bf16[1024,2560]{1,0:T(8,128)(2,1)}, u32[]{:S(2)}, u32[]{:S(2)}) collective-permute-start(bf16[1024,2560]{1,0:T(8,128)(2,1)} %get-tuple-element.132.dp0), channel_id=1, source_target_pairs={{0,1},{1,0},{2,3},{3,2},{4,5},{5,4},{6,7},{7,6}} | collective-permute-start | bytes 15728648 | tf_op jit(solution)/shard_map/ppermute | solution.py:784
  704.7 162.3 %collective-permute-start.17 = (bf16[2048,2560]{1,0:T(8,128)(2,1)}, bf16[2048,2560]{1,0:T(8,128)(2,1)}, u32[]{:S(2)}, u32[]{:S(2)}) collective-permute-start(bf16[2048,2560]{1,0:T(8,128)(2,1)} %get-tuple-element.129.dm_o.own_ref), channel_id=1, source_target_pairs={{0,1},{1,0},{2,3},{3,2},{4,5},{5,4},{6,7},{7,6}} | collective-permute-start | bytes 31457288 | tf_op jit(solution)/shard_map/ppermute | solution.py:784
  728.5 59.2 %collective-permute-start.22 = (bf16[512,2560]{1,0:T(8,128)(2,1)}, bf16[512,2560]{1,0:T(8,128)(2,1)}, u32[]{:S(2)}, u32[]{:S(2)}) collective-permute-start(bf16[512,2560]{1,0:T(8,128)(2,1)} %get-tuple-element.134), channel_id=1, source_target_pairs={{0,2},{2,0},{1,3},{3,1},{4,6},{6,4},{5,7},{7,5}} | collective-permute-start | bytes 7864328 | tf_op jit(solution)/shard_map/ppermute | solution.py:784
  729.6 77.8 %collective-permute-start.15 = (bf16[1024,1152]{1,0:T(8,128)(2,1)}, bf16[1024,1152]{1,0:T(8,128)(2,1)}, u32[]{:S(2)}, u32[]{:S(2)}) collective-permute-start(bf16[1024,1152]{1,0:T(8,128)(2,1)} %get-tuple-element.127.n0), channel_id=1, source_target_pairs={{0,1},{1,0},{2,3},{3,2},{4,5},{5,4},{6,7},{7,6}} | collective-permute-start | bytes 7077896 | tf_op jit(solution)/shard_map/ppermute | solution.py:784
  729.6 78.3 %collective-permute-start.16 = (bf16[1024,1152]{1,0:T(8,128)(2,1)}, bf16[1024,1152]{1,0:T(8,128)(2,1)}, u32[]{:S(2)}, u32[]{:S(2)}) collective-permute-start(bf16[1024,1152]{1,0:T(8,128)(2,1)} %get-tuple-element.128.n2), channel_id=1, source_target_pairs={{0,1},{1,0},{2,3},{3,2},{4,5},{5,4},{6,7},{7,6}} | collective-permute-start | bytes 7077896 | tf_op jit(solution)/shard_map/ppermute | solution.py:784
  730.7 78.3 %copy-start.21 = (pred[16]{0:T(512)(128)(4,1)S(1)}, pred[16]{0:T(512)(128)(4,1)}, u32[]{:S(2)}) copy-start(pred[16]{0:T(512)(128)(4,1)} %copy-done.20) | copy-start | bytes 52
  730.7 78.4 %copy-start.19 = (pred[16]{0:T(512)(128)(4,1)S(1)}, pred[16]{0:T(512)(128)(4,1)}, u32[]{:S(2)}) copy-start(pred[16]{0:T(512)(128)(4,1)} %copy-done.18) | copy-start | bytes 52
  730.7 78.5 %copy-start.13 = (s32[16]{0:T(128)S(1)}, s32[16]{0:T(128)}, u32[]{:S(2)}) copy-start(s32[16]{0:T(128)} %copy-done.12) | copy-start | bytes 196
  730.7 78.6 %copy-start.11 = (s32[16]{0:T(128)S(1)}, s32[16]{0:T(128)}, u32[]{:S(2)}) copy-start(s32[16]{0:T(128)} %copy-done.10) | copy-start | bytes 196
  730.7 78.7 %copy-start.3 = (s32[8]{0:T(128)S(1)}, s32[8]{0:T(128)}, u32[]{:S(2)}) copy-start(s32[8]{0:T(128)} %param.16) | copy-start | bytes 100
  730.7 79.7 %collective-permute-start.23 = (bf16[512,2560]{1,0:T(8,128)(2,1)}, bf16[512,2560]{1,0:T(8,128)(2,1)}, u32[]{:S(2)}, u32[]{:S(2)}) collective-permute-start(bf16[512,2560]{1,0:T(8,128)(2,1)} %get-tuple-element.134), channel_id=1, source_target_pairs={{0,1},{1,0},{2,3},{3,2},{4,5},{5,4},{6,7},{7,6}} | collective-permute-start | bytes 7864328 | tf_op jit(solution)/shard_map/ppermute | solution.py:784
  787.7 22.8 %collective-permute-start.24 = (bf16[512,2560]{1,0:T(8,128)(2,1)}, bf16[512,2560]{1,0:T(8,128)(2,1)}, u32[]{:S(2)}, u32[]{:S(2)}) collective-permute-start(bf16[512,2560]{1,0:T(8,128)(2,1)} %collective-permute-done.22.go_x), channel_id=1, source_target_pairs={{0,1},{1,0},{2,3},{3,2},{4,5},{5,4},{6,7},{7,6}} | collective-permute-start | bytes 7864328 | tf_op jit(solution)/shard_map/ppermute | solution.py:784
  807.4 5.4 collective-permute-start.19
  807.9 59.1 %collective-permute-start.18 = (bf16[640,2048]{1,0:T(8,128)(2,1)}, bf16[640,2048]{1,0:T(8,128)(2,1)}, u32[]{:S(2)}, u32[]{:S(2)}) collective-permute-start(bf16[640,2048]{1,0:T(8,128)(2,1)} %get-tuple-element.131), channel_id=1, source_target_pairs={{0,2},{2,0},{1,3},{3,1},{4,6},{6,4},{5,7},{7,5}} | collective-permute-start | bytes 7864328 | tf_op jit(solution)/shard_map/ppermute | solution.py:784
  904.9 38.0 %copy-start.5 = (f32[1,2560]{1,0:T(1,128)S(1)}, f32[1,2560]{1,0:T(1,128)}, u32[]{:S(2)}) copy-start(f32[1,2560]{1,0:T(1,128)} %get-tuple-element.157) | copy-start | bytes 30724
  904.9 38.0 %copy-start.6 = (f32[1,2560]{1,0:T(1,128)S(1)}, f32[1,2560]{1,0:T(1,128)}, u32[]{:S(2)}) copy-start(f32[1,2560]{1,0:T(1,128)} %get-tuple-element.156) | copy-start | bytes 30724
  904.9 38.0 %copy-start.15 = (f32[1,256]{1,0:T(1,128)S(1)}, f32[1,256]{1,0:T(1,128)}, u32[]{:S(2)}) copy-start(f32[1,256]{1,0:T(1,128)} %get-tuple-element.153) | copy-start | bytes 3076
  904.9 38.0 %copy-start.17 = (f32[1,256]{1,0:T(1,128)S(1)}, f32[1,256]{1,0:T(1,128)}, u32[]{:S(2)}) copy-start(f32[1,256]{1,0:T(1,128)} %get-tuple-element.152) | copy-start | bytes 3076
  905.0 38.0 %copy-start.14 = (f32[1,256]{1,0:T(1,128)S(1)}, f32[1,256]{1,0:T(1,128)}, u32[]{:S(2)}) copy-start(f32[1,256]{1,0:T(1,128)} %get-tuple-element.155) | copy-start | bytes 3076
  905.0 38.0 %copy-start.16 = (f32[1,256]{1,0:T(1,128)S(1)}, f32[1,256]{1,0:T(1,128)}, u32[]{:S(2)}) copy-start(f32[1,256]{1,0:T(1,128)} %get-tuple-element.154) | copy-start | bytes 3076
  905.0 49.8 %copy-start.9 = (f32[1,1152]{1,0:T(1,128)S(1)}, f32[1,1152]{1,0:T(1,128)}, u32[]{:S(2)}) copy-start(f32[1,1152]{1,0:T(1,128)} %get-tuple-element.146) | copy-start | bytes 13828
  905.0 53.4 %copy-start.4 = (f32[1,2560]{1,0:T(1,128)S(1)}, f32[1,2560]{1,0:T(1,128)}, u32[]{:S(2)}) copy-start(f32[1,2560]{1,0:T(1,128)} %get-tuple-element.148) | copy-start | bytes 30724
  905.0 56.4 %collective-permute-start.25 = (bf16[1152,1280]{1,0:T(8,128)(2,1)}, bf16[1152,1280]{1,0:T(8,128)(2,1)}, u32[]{:S(2)}, u32[]{:S(2)}) collective-permute-start(bf16[1152,1280]{1,0:T(8,128)(2,1)} %get-tuple-element.138), channel_id=1, source_target_pairs={{0,1},{1,0},{2,3},{3,2},{4,5},{5,4},{6,7},{7,6}} | collective-permute-start | bytes 8847368 | tf_op jit(solution)/shard_map/ppermute | solution.py:784
  941.8 19.6 %collective-permute-start.26 = (bf16[1280,1024]{1,0:T(8,128)(2,1)}, bf16[1280,1024]{1,0:T(8,128)(2,1)}, u32[]{:S(2)}, u32[]{:S(2)}) collective-permute-start(bf16[1280,1024]{1,0:T(8,128)(2,1)} %get-tuple-element.139), channel_id=1, source_target_pairs={{0,1},{1,0},{2,3},{3,2},{4,5},{5,4},{6,7},{7,6}} | collective-permute-start | bytes 7864328 | tf_op jit(solution)/shard_map/ppermute | solution.py:784
  942.4 19.0 %collective-permute-start.27 = (bf16[1280,1024]{1,0:T(8,128)(2,1)}, bf16[1280,1024]{1,0:T(8,128)(2,1)}, u32[]{:S(2)}, u32[]{:S(2)}) collective-permute-start(bf16[1280,1024]{1,0:T(8,128)(2,1)} %get-tuple-element.140), channel_id=1, source_target_pairs={{0,1},{1,0},{2,3},{3,2},{4,5},{5,4},{6,7},{7,6}} | collective-permute-start | bytes 7864328 | tf_op jit(solution)/shard_map/ppermute | solution.py:784
  942.4 19.0 %collective-permute-start.28 = (bf16[640,2048]{1,0:T(8,128)(2,1)}, bf16[640,2048]{1,0:T(8,128)(2,1)}, u32[]{:S(2)}, u32[]{:S(2)}) collective-permute-start(bf16[640,2048]{1,0:T(8,128)(2,1)} %collective-permute-done.18.gq_x), channel_id=1, source_target_pairs={{0,1},{1,0},{2,3},{3,2},{4,5},{5,4},{6,7},{7,6}} | collective-permute-start | bytes 7864328 | tf_op jit(solution)/shard_map/ppermute | solution.py:784
  943.0 11.8 %collective-permute-start.32 = (f32[1,3072]{1,0:T(1,128)S(1)}, f32[1,3072]{1,0:T(1,128)S(1)}, u32[]{:S(2)}, u32[]{:S(2)}) collective-permute-start(f32[1,3072]{1,0:T(1,128)S(1)} %pad_maximum_fusion.1), channel_id=1, source_target_pairs={{0,1},{1,0},{2,3},{3,2},{4,5},{5,4},{6,7},{7,6}} | collective-permute-start | bytes 36872 | tf_op jit(solution)/shard_map/ppermute | solution.py:784
  954.8 3.6 collective-permute-start.29
  958.4 1.2 collective-permute-start.31
  959.6 1.2 collective-permute-start.30
